TPU v7x, 32 devices: a whole 2x2x4 slice. The times are simulated.
32 devices in a mesh: rep: 2 (over core), row: 16 (over z, y, x).
Axes of the slice: x: 2, y: 2, z: 4, core: 2. Of those that a mesh axis runs over, the one named last changes fastest.
Arguments:
- tiles: bfloat16 [128, 16, 128, 128], P('row', 'rep'), as said below
- tile_cols: int32 [128, 16], replicated, may hold values from -1 to 127, as said below
Outputs:
- vertex_counts: float32 [128, 128], P('row', 'rep')
Inputs may be any that keep to these rules, and one draw needn't show every extreme that they name: `tile_cols`: in each tile row I the filled slots come first and hold distinct tile columns from I - 32 to I, in increasing order; empty slots hold -1. At most 16 slots of a row are filled, and some row has all 16 filled. `tiles`: tiles of empty slots are zero; a tile on the diagonal (column equal to row) is zero on and above its own diagonal.
All inputs are finite; a program needn't handle non-finite values.
Results may differ from a plain program's by a relative error of at most 0.0003.
Values may be sent and summed in bfloat16 or wider, within the bound.
No kernel may reach another device: no remote copies, remote signals or barrier semaphores. Data moves between devices by JAX's collectives and lax.ppermute only.
A program may use at most 128 MiB of HBM per device.

v0:
```python
import jax
import jax.numpy as jnp
from jax import lax
from jax.experimental import pallas as pl
from jax.experimental.pallas import tpu as pltpu
from jax.sharding import PartitionSpec as P


BACK = 4
UNROLL = 8
(OWN, SIDE0, SIDE1, NEXT, UP3, UP) = range(6)
(SIDE_NEXT0, SIDE_NEXT1, SIDE_UP, NEXT_UP, UP3_DIAG, UP_DOWN) = range(6, 12)
GROUPS = 12
SPLIT = (SIDE0, SIDE_NEXT0)
ARRIVES = (
    (UP3_DIAG, NEXT_UP, UP_DOWN, UP),
    (SIDE0, NEXT_UP, UP_DOWN, UP),
    (SIDE_NEXT0, NEXT, SIDE_UP, UP),
    (SIDE0, NEXT, SIDE_NEXT0, UP3),
)


def swap_cores(x):
    return lax.ppermute(x, "rep", [(0, 1), (1, 0)])


def moved(x, steps):
    size = lax.axis_size("row")
    route = [(i, i + steps[i % BACK]) for i in range(size) if i % BACK in steps]
    return lax.ppermute(x, "row", [(i, j) for i, j in route if j < size])


def running(flags):
    n = flags.shape[-1]
    tri = (jnp.arange(n)[:, None] < jnp.arange(n)[None, :]).astype(jnp.bfloat16)
    flat = flags.reshape(-1, n).astype(jnp.bfloat16)
    count = jnp.dot(flat, tri, preferred_element_type=jnp.float32)
    return count.astype(jnp.int32).reshape(flags.shape)


def send_lists(tile_cols, rows):
    count, slots = tile_cols.shape
    blocks = count // rows
    every = jnp.arange(count, dtype=jnp.int32)
    hot = tile_cols[:, :, None] == every
    member = jnp.any(hot, axis=1).astype(jnp.bfloat16).reshape(blocks, rows, count)
    padded = jnp.pad(member, ((0, BACK), (0, 0), (0, 0)))
    later = jnp.concatenate([padded[d : d + blocks] for d in range(1, BACK + 1)], axis=1)
    column = hot.reshape(blocks, rows * slots, count).astype(jnp.bfloat16)
    line = jnp.broadcast_to((every[:, None] == every)[:, None, :], hot.shape)
    line = line.reshape(blocks, rows * slots, count).astype(jnp.bfloat16)
    dims = (((2,), (2,)), ((0,), (0,)))
    has_column = lax.dot_general(later, column, dims, preferred_element_type=jnp.float32)
    has_line = lax.dot_general(later, line, dims, preferred_element_type=jnp.float32)
    both = (has_column * has_line).reshape(blocks, BACK, rows, rows * slots)
    need = jnp.max(both, axis=2) > 0
    place = (jnp.arange(blocks) % BACK)[:, None]
    near, second, third, fourth = (need[:, d] for d in range(BACK))
    side = (near & (place != 3)) | (third & ((place == 0) | (place == 3)))
    upper = fourth | (near & (place == 3)) | (third & ((place == 1) | (place == 2)))
    lists = jnp.stack([side, second, upper], axis=1)
    ahead = side & third & ((place == 0) | (place == 3))
    order = running(jnp.concatenate([lists, ahead[:, None]], axis=1))
    first = order[:, 3]
    total = jnp.sum(ahead.astype(jnp.int32), axis=1, keepdims=True)
    side_rank = jnp.where(ahead, first, order[:, 0] - first + total)
    ranks = jnp.concatenate([side_rank[:, None], order[:, 1:3]], axis=1)
    return lists, ranks, total[:, 0]


def gather_kernel(pieces, index_ref, mine_ref, other_ref, *rest):
    outs, pool, sem = rest[:-2], rest[-2], rest[-1]
    half = mine_ref.shape[0]
    first = pltpu.make_async_copy(mine_ref, pool.at[pl.ds(0, half)], sem.at[0])
    second = pltpu.make_async_copy(other_ref, pool.at[pl.ds(half, half)], sem.at[1])
    first.start()
    second.start()
    first.wait()
    second.wait()
    for out, (which, start, cap) in zip(outs, pieces):

        def one(p, carry, out=out, which=which, start=start):
            out[p] = pool[index_ref[which, start + p]]
            return carry

        lax.fori_loop(0, cap, one, 0, unroll=2)


def gather_tiles(pieces, index, mine, other):
    tile = mine.shape[-2:]
    anywhere = pl.BlockSpec(memory_space=pl.ANY)
    total = sum(cap for _, _, cap in pieces)
    return pl.pallas_call(
        lambda *refs: gather_kernel(pieces, *refs),
        out_shape=[jax.ShapeDtypeStruct((cap,) + tile, mine.dtype) for _, _, cap in pieces],
        in_specs=[pl.BlockSpec(memory_space=pltpu.SMEM), anywhere, anywhere],
        out_specs=[pl.BlockSpec(memory_space=pltpu.VMEM)] * len(pieces),
        scratch_shapes=[
            pltpu.VMEM((2 * mine.shape[0],) + tile, mine.dtype),
            pltpu.SemaphoreType.DMA((2,)),
        ],
        cost_estimate=pl.CostEstimate(
            flops=10**6, bytes_accessed=total * 65536, transcendentals=0
        ),
    )(index, mine, other)


def count_kernel(groups, rows, start_ref, item_ref, before_ref, mine_ref, other_ref, *rest):
    n = len(groups)
    bufs, out_ref, own, acc = rest[:n], rest[n], rest[n + 1], rest[n + 2]
    held, sem, own_sem = rest[n + 3 : 2 * n + 3], rest[-2], rest[-1]
    half = mine_ref.shape[0]
    slots_here = half // rows
    first = pltpu.make_async_copy(mine_ref, own.at[pl.ds(0, half)], own_sem.at[0])
    second = pltpu.make_async_copy(other_ref, own.at[pl.ds(half, half)], own_sem.at[1])
    first.start()
    second.start()
    for i, group in enumerate(groups):

        @pl.when(start_ref[0, group + 1] > start_ref[0, group])
        def _(i=i):
            pltpu.make_async_copy(bufs[i], held[i], sem.at[i]).start()

    own[2 * half] = jnp.zeros(own.shape[1:], own.dtype)
    acc[...] = jnp.zeros_like(acc)
    first.wait()
    second.wait()

    def work(group, source):
        def step(i, carry):
            for u in range(UNROLL):
                n = i * UNROLL + u
                code = item_ref[n >> 7, n & 127]
                a = code & 255
                b = (code >> 8) & 255
                t = code >> 16
                row = (a & (half - 1)) // slots_here
                product = jnp.dot(own[a], source[t], preferred_element_type=jnp.float32)
                acc[row] += product * own[b].astype(jnp.float32)
            return carry

        lax.fori_loop(start_ref[0, group], start_ref[0, group + 1], step, 0)

    if not groups:
        work(OWN, own)
    for i, group in enumerate(groups):

        @pl.when(start_ref[0, group + 1] > start_ref[0, group])
        def _(i=i, group=group):
            pltpu.make_async_copy(bufs[i], held[i], sem.at[i]).wait()
            work(group, held[i])

    out_ref[...] = before_ref[...] + jnp.sum(acc[...], axis=2)


def count_tiles(groups, rows, starts, items, before, mine, other, bufs, flops):
    half, tile, _ = mine.shape
    anywhere = pl.BlockSpec(memory_space=pl.ANY)
    vmem = pl.BlockSpec(memory_space=pltpu.VMEM)
    return pl.pallas_call(
        lambda *refs: count_kernel(groups, rows, *refs),
        out_shape=jax.ShapeDtypeStruct((rows, tile), jnp.float32),
        in_specs=[pl.BlockSpec(memory_space=pltpu.SMEM)] * 2 + [vmem] + [anywhere] * (2 + len(bufs)),
        out_specs=vmem,
        scratch_shapes=[
            pltpu.VMEM((2 * half + 1, tile, tile), mine.dtype),
            pltpu.VMEM((rows, tile, tile), jnp.float32),
        ]
        + [pltpu.VMEM(b.shape, b.dtype) for b in bufs]
        + [pltpu.SemaphoreType.DMA((max(1, len(bufs)),)), pltpu.SemaphoreType.DMA((2,))],
        cost_estimate=pl.CostEstimate(flops=flops, bytes_accessed=8 * 10**6, transcendentals=0),
    )(starts, items, before, mine, other, *bufs)


def list_kernel(cut, half, near_ref, spot_ref, row_ref, column_ref, group_ref, a_ref, b_ref, start_ref, item_ref):
    slots, lanes = near_ref.shape
    f32, bf16 = jnp.float32, jnp.bfloat16
    down = lax.broadcasted_iota(jnp.int32, (lanes, lanes), 0)
    across = lax.broadcasted_iota(jnp.int32, (lanes, lanes), 1)

    where = jnp.zeros((lanes, lanes), jnp.int32)
    for s in range(slots):
        where = where + jnp.where(down == near_ref[s : s + 1], spot_ref[s : s + 1], 0)
    line = (down == row_ref[...]).astype(bf16)
    where = jnp.dot(where.astype(bf16), line, preferred_element_type=f32)
    column = (across == column_ref[...]).astype(bf16)
    found = jnp.dot(column, where.astype(bf16), preferred_element_type=f32)
    found = jnp.where(down // slots == across // slots, found, 0.0).astype(bf16)
    fold = lax.broadcasted_iota(jnp.int32, (slots, lanes), 0)
    fold = fold == lax.broadcasted_iota(jnp.int32, (slots, lanes), 1) % slots
    found = jnp.dot(fold.astype(bf16), found, preferred_element_type=f32).astype(jnp.int32)

    group = jnp.broadcast_to(group_ref[...], found.shape)
    for split in SPLIT:
        second = (group_ref[...] == split) & (found > cut)
        group = jnp.where(second, split + 1, group)
        found = jnp.where(second, found - cut, found)

    chosen = [((group == g) & (found > 0)).astype(f32) for g in range(GROUPS)]
    stack = jnp.concatenate(chosen, axis=0).astype(bf16)
    before = (down < across).astype(bf16)
    rank = jnp.dot(stack, before, preferred_element_type=f32)
    sums = jnp.dot(stack, jnp.ones((lanes, lanes), bf16), preferred_element_type=f32)
    above = lax.broadcasted_iota(jnp.int32, (slots, slots), 0)
    above = (above > lax.broadcasted_iota(jnp.int32, (slots, slots), 1)).astype(bf16)
    start = jnp.zeros((1, lanes), f32)
    target = jnp.zeros((slots, lanes), f32)
    starts = jnp.zeros(start_ref.shape, f32)
    lane = lax.broadcasted_iota(jnp.int32, start_ref.shape, 1)
    for g in range(GROUPS):
        part = slice(g * slots, (g + 1) * slots)
        ahead = jnp.dot(above, sums[part].astype(bf16), preferred_element_type=f32)
        place = rank[part] + ahead + start * UNROLL + 1.0
        target = target + chosen[g] * place
        trips = jnp.floor((jnp.sum(sums[part], axis=0, keepdims=True) + (UNROLL - 1)) / UNROLL)
        start = start + trips
        starts = jnp.where(lane == g + 1, start, starts)
    start_ref[...] = starts.astype(jnp.int32)

    high = lax.broadcasted_iota(jnp.int32, (item_ref.shape[0], lanes), 0)
    target = target.astype(jnp.int32) - 1
    total = jnp.zeros((3 * item_ref.shape[0], lanes), f32)
    for q in range(slots):
        t = target[q : q + 1]
        major, minor = t >> 7, t & 127
        fields = (a_ref[...], 2 * half - b_ref[q : q + 1], found[q : q + 1] - 1)
        left = [jnp.where(high == major, field, 0).astype(f32) for field in fields]
        left = jnp.concatenate(left, axis=0).astype(bf16)
        right = (down == minor).astype(bf16)
        total = total + lax.dot_general(
            left, right, (((1,), (1,)), ((), ())), preferred_element_type=f32
        )
    total = total.astype(jnp.int32)
    n = item_ref.shape[0]
    item_ref[...] = total[:n] + (2 * half - total[n : 2 * n]) * 256 + total[2 * n :] * 65536


def list_inputs(tile_cols, lists, ranks, rows, here, core, loc):
    _, slots = tile_cols.shape
    per_block = rows * slots
    window = (BACK + 1) * rows
    place = here % BACK

    pad = ((BACK, 0), (0, 0), (0, 0))
    near_lists = lax.dynamic_slice_in_dim(jnp.pad(lists, pad), here, BACK, 0)
    near_ranks = lax.dynamic_slice_in_dim(jnp.pad(ranks, pad), here, BACK, 0)
    from_place = (here + jnp.arange(BACK)) % BACK
    dist = BACK - jnp.arange(BACK)
    upper = (dist == 4) | ((dist == 1) & (from_place == 3))
    upper = upper | ((dist == 3) & ((from_place == 1) | (from_place == 2)))
    which = jnp.where(dist == 2, 1, jnp.where(upper, 2, 0))
    pick = (which[:, None] == jnp.arange(3))[:, :, None]
    flag = jnp.any(near_lists & pick, axis=1)
    rank = jnp.sum(jnp.where(pick, near_ranks, 0), axis=1)
    spot = jnp.where(flag & (rank % 2 == core), rank // 2 + 1, 0)
    order = jnp.arange(per_block, dtype=jnp.int32)
    own_spot = jnp.where(order % 2 == core, loc + 1, 0)
    spot = jnp.concatenate([spot, own_spot[None]], axis=0).reshape(window, slots)

    base = (here - BACK) * rows
    padded = jnp.pad(tile_cols, ((BACK * rows, 0), (0, 0)), constant_values=-1)
    near = lax.dynamic_slice(padded, (here * rows, 0), (window, slots))
    near = jnp.where(near >= 0, near - base, -1)
    mine = near[BACK * rows :]
    back = BACK - mine // rows
    group = jnp.zeros_like(back)
    for row in range(BACK):
        for d in range(1, BACK + 1):
            group = jnp.where((place == row) & (back == d), ARRIVES[row][d - 1], group)
    wide = ((0, 0), (0, per_block - window))
    return (
        jnp.pad(near.T, wide, constant_values=-1),
        jnp.pad(spot.T, wide),
        mine.reshape(1, per_block),
        mine.reshape(per_block, 1),
        group.reshape(1, per_block),
        loc.reshape(1, per_block),
        jnp.repeat(loc.reshape(rows, slots).T, slots, axis=1),
    )


def work_list(inputs, cut, rows, half):
    slots, lanes = inputs[0].shape
    limit = rows * slots * (slots + 1) // 2 + GROUPS * UNROLL
    depth = -(-limit // (8 * lanes)) * 8
    vmem = pl.BlockSpec(memory_space=pltpu.VMEM)
    return pl.pallas_call(
        lambda *refs: list_kernel(cut, half, *refs),
        out_shape=[
            jax.ShapeDtypeStruct((8, lanes), jnp.int32),
            jax.ShapeDtypeStruct((depth, lanes), jnp.int32),
        ],
        in_specs=[vmem] * len(inputs),
        out_specs=[vmem, vmem],
        cost_estimate=pl.CostEstimate(flops=10**9, bytes_accessed=10**5, transcendentals=0),
    )(*inputs)


def body(tiles, tile_cols):
    rows, half_slots, tile, _ = tiles.shape
    _, slots = tile_cols.shape
    core = lax.axis_index("rep")
    here = lax.axis_index("row")
    half = rows * half_slots
    per_block = rows * slots
    mine = tiles.reshape(half, tile, tile)
    other = swap_cores(mine)

    lists, ranks, ahead = send_lists(tile_cols, rows)
    totals = jnp.sum(lists.astype(jnp.int32), axis=2)
    slot = jnp.arange(per_block, dtype=jnp.int32)
    line, column = slot // slots, slot % slots
    loc = ((column // half_slots) ^ core) * half + line * half_slots + column % half_slots

    full = per_block // 2
    my_list = lax.dynamic_index_in_dim(lists, here, 0, False)
    my_rank = lax.dynamic_index_in_dim(ranks, here, 0, False)
    want = (jnp.arange(full, dtype=jnp.int32) * 2 + core)[None, :, None]
    match = my_list[:, None, :] & (my_rank[:, None, :] == want)
    index = jnp.sum(jnp.where(match, loc, 0), axis=2)

    def run(caps):
        cut, rest = caps[0], caps[1]

        def exchange(mine, other, index, inputs):
            pieces = [(0, 0, cut), (1, 0, caps[2]), (2, 0, caps[3]), (2, 0, caps[4])]
            pieces += [(0, cut, rest)] * (rest > 0)
            sent = gather_tiles(pieces, index, mine, other)
            sent, inputs = lax.optimization_barrier((sent, inputs))
            pair = {0: 1, 1: -1, 2: 1, 3: -1}
            side0 = moved(sent[0], pair)
            up3 = moved(sent[2], {3: 4})
            second = moved(sent[1], {0: 2, 1: 2, 2: -2, 3: -2})
            up = moved(sent[3], {0: 4, 1: 4, 2: 4})
            side1 = moved(sent[4], pair) if rest else None
            starts, items = work_list(inputs, cut, rows, half)
            counts = jnp.zeros((rows, tile), jnp.float32)
            counts = count_tiles((), rows, starts, items, counts, mine, other, [], 10**9)
            side0, counts = lax.optimization_barrier((side0, counts))
            side_next0 = moved(side0, {0: 2, 1: 2})
            side_up = moved(side0, {2: 4})
            up_down = moved(up, {1: -1, 2: -1})
            next_up = moved(second, {0: 4, 1: 4})
            up3_diag = moved(up3, {3: -3})
            early = {SIDE0: side0, NEXT: second, UP3: up3, UP: up}
            middle = {SIDE_NEXT0: side_next0, SIDE_UP: side_up, NEXT_UP: next_up, UP_DOWN: up_down}
            late = {UP3_DIAG: up3_diag}
            if rest:
                early[SIDE1] = side1
                late[SIDE_NEXT1] = moved(side1, {0: 2})
            for bufs in (early, middle, late):
                counts = count_tiles(
                    tuple(bufs), rows, starts, items, counts, mine, other, list(bufs.values()), 10**9
                )
            return counts

        return exchange

    place = jnp.arange(totals.shape[0]) % BACK

    def fit(caps):
        upper = jnp.where(place == 3, caps[3], caps[4])
        sizes = jnp.stack([ahead, totals[:, 0], totals[:, 1], totals[:, 2]], axis=1)
        bound = [jnp.full_like(place, c) for c in (caps[0], caps[0] + caps[1], caps[2])] + [upper]
        return jnp.all(sizes <= 2 * jnp.stack(bound, axis=1))

    brief = (full * 7 // 16, full * 5 // 16, full * 5 // 8, full * 11 // 16, full * 15 // 32)
    most = (full, 0, full, full, full)
    inputs = list_inputs(tile_cols, lists, ranks, rows, here, core, loc)
    partial = lax.cond(fit(brief), run(brief), run(most), mine, other, index, inputs)

    width = tile // 2
    keep = lax.dynamic_slice_in_dim(partial, core * width, width, 1)
    give = lax.dynamic_slice_in_dim(partial, (1 - core) * width, width, 1)
    return keep + swap_cores(give)


def solution(mesh):
    return jax.shard_map(
        body,
        mesh=mesh,
        in_specs=(P("row", "rep", None, None), P()),
        out_specs=P("row", "rep"),
        check_vma=False,
    )
```

profile of v0, /device:TPU:25, one launch (start us, length us, event | category | flops | bytes accessed | tf_op | source)
XLA Modules:
  0.0 92.2 jit_solution(551422972887303802)
XLA Ops:
  0.7 0.8 copy.83
  7.0 82.2 %conditional.1 = (f32[8,128]{1,0:T(8,128)S(1)}) conditional(s32[]{:T(128)} %convert_element_type.28, (s32[3,64]{1,0:T(4,128)S(1)}, bf16[64,128,128]{2,1,0:T(8,128)(2,1)S(1)}, bf16[64,128,128]{2,1,0:T(8,128)(2,1)}, s32[16,128]{1,0:T(8,128)S(1)}, s32[16,128]{0,1:T(8,128)S(1)}, /*index=5*/s32[1,128]{1,0:T(1,128)S(1)}, s32[128,1]{0,1:T(1,128)S(1)}, ...), branch_computations={%region_8.9_spmd, %region_9.10_spmd} | conditional | flops 5000999936 | bytes 124396568 | solution.py:370
  8.4 5.5 %branch_1_fun.6 = (bf16[28,128,128]{2,1,0:T(8,128)(2,1)}, bf16[40,128,128]{2,1,0:T(8,128)(2,1)}, bf16[44,128,128]{2,1,0:T(8,128)(2,1)}, bf16[30,128,128]{2,1,0:T(8,128)(2,1)}, bf16[20,128,128]{2,1,0:T(8,128)(2,1)}) custom-call(s32[3,64]{1,0:T(4,128)S(1)} %get-tuple-element.77.refs_0_, bf16[64,128,128]{2,1,0:T(8,128)(2,1)S(1)} %get-tuple-element.78.refs_1_.refs_3_, ...), custom_call_target="tpu_custom_call" | custom-call | flops 1000000 | bytes 10616832 | tf_op jit(solution)/shard_map/cond/branch_1_fun/pallas_call | solution.py:93
  14.8 1.3 %collective-permute-start.10 = (bf16[40,128,128]{2,1,0:T(8,128)(2,1)}, bf16[40,128,128]{2,1,0:T(8,128)(2,1)}, u32[]{:S(2)}, u32[]{:S(2)}) collective-permute-start(bf16[40,128,128]{2,1,0:T(8,128)(2,1)} %get-tuple-element.104), channel_id=1, source_target_pairs={{0,2},{1,3},{2,0},{3,1},{4,6},{5,7},{6,4},{7,5},{8,10},{9,11},{10,... | collective-permute-start | bytes 3932168 | tf_op jit(solution)/shard_map/cond/branch_1_fun/ppermute | solution.py:30
  16.1 1.8 %collective-permute-start.9 = (bf16[28,128,128]{2,1,0:T(8,128)(2,1)}, bf16[28,128,128]{2,1,0:T(8,128)(2,1)}, u32[]{:S(2)}, u32[]{:S(2)}) collective-permute-start(bf16[28,128,128]{2,1,0:T(8,128)(2,1)} %get-tuple-element.101), channel_id=1, source_target_pairs={{0,1},{1,0},{2,3},{3,2},{4,5},{5,4},{6,7},{7,6},{8,9},{9,8},{10,11... | collective-permute-start | bytes 2752520 | tf_op jit(solution)/shard_map/cond/branch_1_fun/ppermute | solution.py:30
  17.8 1.3 %collective-permute-start.12 = (bf16[30,128,128]{2,1,0:T(8,128)(2,1)}, bf16[30,128,128]{2,1,0:T(8,128)(2,1)}, u32[]{:S(2)}, u32[]{:S(2)}) collective-permute-start(bf16[30,128,128]{2,1,0:T(8,128)(2,1)} %get-tuple-element.106), channel_id=1, source_target_pairs={{0,4},{1,5},{2,6},{4,8},{5,9},{6,10},{8,12},{9,13},{10,14},{16,20}... | collective-permute-start | bytes 2949128 | tf_op jit(solution)/shard_map/cond/branch_1_fun/ppermute | solution.py:30
  19.2 2.8 %branch_1_fun.7 = (s32[8,128]{1,0:T(8,128)}, s32[16,128]{1,0:T(8,128)}) custom-call(s32[16,128]{1,0:T(8,128)} %copy-done.3, s32[16,128]{1,0:T(8,128)} %copy.95.refs_1_, s32[1,128]{1,0:T(1,128)} %copy-done.4, s32[128,1]{1,0:T(8,128)} %copy.96.refs_3_, s32[1,128]{1,0:T(1,128)} %copy-done.5, s32[1,128]{1,0:T(1,128)} %copy-done.6, ...), custom_call_target="tpu_custom_call" | custom-call | flops 1000000000 | bytes 100000 | tf_op jit(solution)/shard_map/cond/branch_1_fun/pallas_call | solution.py:287
  22.6 6.0 %branch_1_fun.8.refs_2_ = f32[8,128]{1,0:T(8,128)} custom-call(s32[8,128]{1,0:T(8,128)} %get-tuple-element.99.refs_0_, s32[16,128]{1,0:T(8,128)} %get-tuple-element.100.refs_1_, f32[8,128]{1,0:T(8,128)} %broadcast_27_refs_2_.0.refs_2_, bf16[64,128,128]{2,1,0:T(8,128)(2,1)S(1)} %get-tuple-element.78.refs_1_.refs_3_, ...), custom_call_target="tpu_custom_call" | custom-call | flops 1000000000 | bytes 8000000 | tf_op jit(solution)/shard_map/cond/branch_1_fun/pallas_call | solution.py:160
  28.6 9.8 %collective-permute-done.9.refs_5_ = bf16[28,128,128]{2,1,0:T(8,128)(2,1)} collective-permute-done((bf16[28,128,128]{2,1,0:T(8,128)(2,1)}, bf16[28,128,128]{2,1,0:T(8,128)(2,1)}, u32[]{:S(2)}, u32[]{:S(2)}) %collective-permute-start.9) | collective-permute-done | bytes 917536 | tf_op jit(solution)/shard_map/cond/branch_1_fun/ppermute | solution.py:30
  38.4 2.8 %collective-permute-start.14 = (bf16[28,128,128]{2,1,0:T(8,128)(2,1)}, bf16[28,128,128]{2,1,0:T(8,128)(2,1)}, u32[]{:S(2)}, u32[]{:S(2)}) collective-permute-start(bf16[28,128,128]{2,1,0:T(8,128)(2,1)} %collective-permute-done.9.refs_5_), channel_id=1, source_target_pairs={{0,2},{1,3},{4,6},{5,7},{8,10},{9,11},{12,14},{13,15},{16,18},{17,... | collective-permute-start | bytes 2752520 | tf_op jit(solution)/shard_map/cond/branch_1_fun/ppermute | solution.py:30
  41.2 1.3 %collective-permute-start.18 = (bf16[44,128,128]{2,1,0:T(8,128)(2,1)S(1)}, bf16[44,128,128]{2,1,0:T(8,128)(2,1)}, u32[]{:S(2)}, u32[]{:S(2)}) collective-permute-start(bf16[44,128,128]{2,1,0:T(8,128)(2,1)S(1)} %collective-permute-done.11.refs_7_), channel_id=1, source_target_pairs={{3,0},{7,4},{11,8},{15,12},{19,16},{23,20},{27,24},{31,28}} | collective-permute-start | bytes 4325384 | tf_op jit(solution)/shard_map/cond/branch_1_fun/ppermute | solution.py:30
  42.5 2.8 %collective-permute-done.10.refs_6_ = bf16[40,128,128]{2,1,0:T(8,128)(2,1)} collective-permute-done((bf16[40,128,128]{2,1,0:T(8,128)(2,1)}, bf16[40,128,128]{2,1,0:T(8,128)(2,1)}, u32[]{:S(2)}, u32[]{:S(2)}) %collective-permute-start.10) | collective-permute-done | bytes 1310752 | tf_op jit(solution)/shard_map/cond/branch_1_fun/ppermute | solution.py:30
  45.3 1.3 %collective-permute-start.16 = (bf16[40,128,128]{2,1,0:T(8,128)(2,1)}, bf16[40,128,128]{2,1,0:T(8,128)(2,1)}, u32[]{:S(2)}, u32[]{:S(2)}) collective-permute-start(bf16[40,128,128]{2,1,0:T(8,128)(2,1)} %collective-permute-done.10.refs_6_), channel_id=1, source_target_pairs={{0,4},{1,5},{4,8},{5,9},{8,12},{9,13},{16,20},{17,21},{20,24},{21,... | collective-permute-start | bytes 3932168 | tf_op jit(solution)/shard_map/cond/branch_1_fun/ppermute | solution.py:30
  46.6 1.3 %collective-permute-start.17 = (bf16[30,128,128]{2,1,0:T(8,128)(2,1)}, bf16[30,128,128]{2,1,0:T(8,128)(2,1)}, u32[]{:S(2)}, u32[]{:S(2)}) collective-permute-start(bf16[30,128,128]{2,1,0:T(8,128)(2,1)} %collective-permute-done.12.refs_8_), channel_id=1, source_target_pairs={{1,0},{2,1},{5,4},{6,5},{9,8},{10,9},{13,12},{14,13},{17,16},{18,1... | collective-permute-start | bytes 2949128 | tf_op jit(solution)/shard_map/cond/branch_1_fun/ppermute | solution.py:30
  47.9 4.5 %collective-permute-done.13.refs_9_ = bf16[20,128,128]{2,1,0:T(8,128)(2,1)} collective-permute-done((bf16[20,128,128]{2,1,0:T(8,128)(2,1)}, bf16[20,128,128]{2,1,0:T(8,128)(2,1)}, u32[]{:S(2)}, u32[]{:S(2)}) %collective-permute-start.13) | collective-permute-done | bytes 655392 | tf_op jit(solution)/shard_map/cond/branch_1_fun/ppermute | solution.py:30
  52.5 1.6 %collective-permute-start.15 = (bf16[28,128,128]{2,1,0:T(8,128)(2,1)}, bf16[28,128,128]{2,1,0:T(8,128)(2,1)}, u32[]{:S(2)}, u32[]{:S(2)}) collective-permute-start(bf16[28,128,128]{2,1,0:T(8,128)(2,1)} %collective-permute-done.9.refs_5_), channel_id=1, source_target_pairs={{2,6},{6,10},{10,14},{18,22},{22,26},{26,30}} | collective-permute-start | bytes 2752520 | tf_op jit(solution)/shard_map/cond/branch_1_fun/ppermute | solution.py:30
  54.1 10.0 %collective-permute-done.14.refs_5_ = bf16[28,128,128]{2,1,0:T(8,128)(2,1)} collective-permute-done((bf16[28,128,128]{2,1,0:T(8,128)(2,1)}, bf16[28,128,128]{2,1,0:T(8,128)(2,1)}, u32[]{:S(2)}, u32[]{:S(2)}) %collective-permute-start.14) | collective-permute-done | bytes 917536 | tf_op jit(solution)/shard_map/cond/branch_1_fun/ppermute | solution.py:30
  64.0 5.0 %collective-permute-start.19 = (bf16[20,128,128]{2,1,0:T(8,128)(2,1)}, bf16[20,128,128]{2,1,0:T(8,128)(2,1)}, u32[]{:S(2)}, u32[]{:S(2)}) collective-permute-start(bf16[20,128,128]{2,1,0:T(8,128)(2,1)} %collective-permute-done.13.refs_9_), channel_id=1, source_target_pairs={{0,2},{4,6},{8,10},{12,14},{16,18},{20,22},{24,26},{28,30}} | collective-permute-start | bytes 1966088 | tf_op jit(solution)/shard_map/cond/branch_1_fun/ppermute | solution.py:30
  69.0 3.9 %branch_1_fun.9.refs_2_ = f32[8,128]{1,0:T(8,128)} custom-call(s32[8,128]{1,0:T(8,128)} %get-tuple-element.99.refs_0_, s32[16,128]{1,0:T(8,128)} %get-tuple-element.100.refs_1_, f32[8,128]{1,0:T(8,128)} %branch_1_fun.8.refs_2_, bf16[64,128,128]{2,1,0:T(8,128)(2,1)S(1)} %get-tuple-element.78.refs_1_.refs_3_, ...), custom_call_target="tpu_custom_call" | custom-call | flops 1000000000 | bytes 8000000 | tf_op jit(solution)/shard_map/cond/branch_1_fun/pallas_call | solution.py:160
  73.5 3.3 %collective-permute-done.16.refs_7_ = bf16[40,128,128]{2,1,0:T(8,128)(2,1)} collective-permute-done((bf16[40,128,128]{2,1,0:T(8,128)(2,1)}, bf16[40,128,128]{2,1,0:T(8,128)(2,1)}, u32[]{:S(2)}, u32[]{:S(2)}) %collective-permute-start.16) | collective-permute-done | bytes 1310752 | tf_op jit(solution)/shard_map/cond/branch_1_fun/ppermute | solution.py:30
  76.8 6.2 %branch_1_fun.10.refs_2_ = f32[8,128]{1,0:T(8,128)} custom-call(s32[8,128]{1,0:T(8,128)} %get-tuple-element.99.refs_0_, s32[16,128]{1,0:T(8,128)} %get-tuple-element.100.refs_1_, f32[8,128]{1,0:T(8,128)} %branch_1_fun.9.refs_2_, bf16[64,128,128]{2,1,0:T(8,128)(2,1)S(1)} %get-tuple-element.78.refs_1_.refs_3_, ...), custom_call_target="tpu_custom_call" | custom-call | flops 1000000000 | bytes 8000000 | tf_op jit(solution)/shard_map/cond/branch_1_fun/pallas_call | solution.py:160
  83.8 5.4 %branch_1_fun.11 = f32[8,128]{1,0:T(8,128)S(1)} custom-call(s32[8,128]{1,0:T(8,128)} %get-tuple-element.99.refs_0_, s32[16,128]{1,0:T(8,128)} %get-tuple-element.100.refs_1_, f32[8,128]{1,0:T(8,128)} %branch_1_fun.10.refs_2_, bf16[64,128,128]{2,1,0:T(8,128)(2,1)S(1)} %get-tuple-element.78.refs_1_.refs_3_, ...), custom_call_target="tpu_custom_call" | custom-call | flops 1000000000 | bytes 8000000 | tf_op jit(solution)/shard_map/cond/branch_1_fun/pallas_call | solution.py:160
  89.2 1.5 %collective-permute-start.21 = (f32[8,64]{1,0:T(8,128)S(1)}, f32[8,64]{1,0:T(8,128)S(1)}, u32[]{:S(2)}, u32[]{:S(2)}) collective-permute-start(f32[8,64]{1,0:T(8,128)S(1)} %constant_dynamic-slice_fusion), channel_id=1, source_target_pairs={{0,16},{16,0},{1,17},{17,1},{2,18},{18,2},{3,19},{19,3},{4,20},{20... | collective-permute-start | bytes 6152 | tf_op jit(solution)/shard_map/ppermute | solution.py:24
  90.7 0.8 collective-permute-done.21
  (82 shorter events, 10.2 us)
Async XLA Ops:
  0.0 7.0 %copy-start = (bf16[8,8,128,128]{3,2,1,0:T(8,128)(2,1)S(1)}, bf16[8,8,128,128]{3,2,1,0:T(8,128)(2,1)}, u32[]{:S(2)}) copy-start(bf16[8,8,128,128]{3,2,1,0:T(8,128)(2,1)} %param.4) | copy-start | bytes 6291460
  0.0 3.9 %copy-start.2 = (s32[128,16]{0,1:T(8,128)S(1)}, s32[128,16]{0,1:T(8,128)}, u32[]{:S(2)}) copy-start(s32[128,16]{0,1:T(8,128)} %param.5) | copy-start | bytes 24580
  0.0 7.0 %collective-permute-start.20 = (bf16[64,128,128]{2,1,0:T(8,128)(2,1)}, bf16[64,128,128]{2,1,0:T(8,128)(2,1)}, u32[]{:S(2)}, u32[]{:S(2)}) collective-permute-start(bf16[64,128,128]{2,1,0:T(8,128)(2,1)} %bitcast.43), channel_id=1, source_target_pairs={{0,16},{16,0},{1,17},{17,1},{2,18},{18,2},{3,19},{19,3},{4,20},{20... | collective-permute-start | bytes 6291464 | tf_op jit(solution)/shard_map/ppermute | solution.py:24
  7.0 7.0 %copy-start.3 = (s32[16,128]{1,0:T(8,128)}, s32[16,128]{1,0:T(8,128)S(1)}, u32[]{:S(2)}) copy-start(s32[16,128]{1,0:T(8,128)S(1)} %get-tuple-element.92.refs_0_) | copy-start | bytes 24580 | tf_op jit(solution)/shard_map/cond
  7.0 7.0 %copy-start.6 = (s32[1,128]{1,0:T(1,128)}, s32[1,128]{1,0:T(1,128)S(1)}, u32[]{:S(2)}) copy-start(s32[1,128]{1,0:T(1,128)S(1)} %get-tuple-element.97.refs_5_) | copy-start | bytes 1540 | tf_op jit(solution)/shard_map/cond
  7.0 7.0 %copy-start.4 = (s32[1,128]{1,0:T(1,128)}, s32[1,128]{1,0:T(1,128)S(1)}, u32[]{:S(2)}) copy-start(s32[1,128]{1,0:T(1,128)S(1)} %get-tuple-element.94.refs_2_) | copy-start | bytes 1540 | tf_op jit(solution)/shard_map/cond
  7.0 7.0 %copy-start.5 = (s32[1,128]{1,0:T(1,128)}, s32[1,128]{1,0:T(1,128)S(1)}, u32[]{:S(2)}) copy-start(s32[1,128]{1,0:T(1,128)S(1)} %get-tuple-element.96.refs_4_) | copy-start | bytes 1540 | tf_op jit(solution)/shard_map/cond
  14.0 27.2 %collective-permute-start.11 = (bf16[44,128,128]{2,1,0:T(8,128)(2,1)}, bf16[44,128,128]{2,1,0:T(8,128)(2,1)S(1)}, u32[]{:S(2)}, u32[]{:S(2)}) collective-permute-start(bf16[44,128,128]{2,1,0:T(8,128)(2,1)} %get-tuple-element.105), channel_id=1, source_target_pairs={{3,7},{7,11},{11,15},{19,23},{23,27},{27,31}} | collective-permute-start | bytes 4325384 | tf_op jit(solution)/shard_map/cond/branch_1_fun/ppermute | solution.py:30
  14.8 30.6 %collective-permute-start.10 = (bf16[40,128,128]{2,1,0:T(8,128)(2,1)}, bf16[40,128,128]{2,1,0:T(8,128)(2,1)}, u32[]{:S(2)}, u32[]{:S(2)}) collective-permute-start(bf16[40,128,128]{2,1,0:T(8,128)(2,1)} %get-tuple-element.104), channel_id=1, source_target_pairs={{0,2},{1,3},{2,0},{3,1},{4,6},{5,7},{6,4},{7,5},{8,10},{9,11},{10,... | collective-permute-start | bytes 3932168 | tf_op jit(solution)/shard_map/cond/branch_1_fun/ppermute | solution.py:30
  16.1 22.3 %collective-permute-start.9 = (bf16[28,128,128]{2,1,0:T(8,128)(2,1)}, bf16[28,128,128]{2,1,0:T(8,128)(2,1)}, u32[]{:S(2)}, u32[]{:S(2)}) collective-permute-start(bf16[28,128,128]{2,1,0:T(8,128)(2,1)} %get-tuple-element.101), channel_id=1, source_target_pairs={{0,1},{1,0},{2,3},{3,2},{4,5},{5,4},{6,7},{7,6},{8,9},{9,8},{10,11... | collective-permute-start | bytes 2752520 | tf_op jit(solution)/shard_map/cond/branch_1_fun/ppermute | solution.py:30
  17.8 28.8 %collective-permute-start.12 = (bf16[30,128,128]{2,1,0:T(8,128)(2,1)}, bf16[30,128,128]{2,1,0:T(8,128)(2,1)}, u32[]{:S(2)}, u32[]{:S(2)}) collective-permute-start(bf16[30,128,128]{2,1,0:T(8,128)(2,1)} %get-tuple-element.106), channel_id=1, source_target_pairs={{0,4},{1,5},{2,6},{4,8},{5,9},{6,10},{8,12},{9,13},{10,14},{16,20}... | collective-permute-start | bytes 2949128 | tf_op jit(solution)/shard_map/cond/branch_1_fun/ppermute | solution.py:30
  19.1 33.4 %collective-permute-start.13 = (bf16[20,128,128]{2,1,0:T(8,128)(2,1)}, bf16[20,128,128]{2,1,0:T(8,128)(2,1)}, u32[]{:S(2)}, u32[]{:S(2)}) collective-permute-start(bf16[20,128,128]{2,1,0:T(8,128)(2,1)} %get-tuple-element.107), channel_id=1, source_target_pairs={{0,1},{1,0},{2,3},{3,2},{4,5},{5,4},{6,7},{7,6},{8,9},{9,8},{10,11... | collective-permute-start | bytes 1966088 | tf_op jit(solution)/shard_map/cond/branch_1_fun/ppermute | solution.py:30
  38.4 25.6 %collective-permute-start.14 = (bf16[28,128,128]{2,1,0:T(8,128)(2,1)}, bf16[28,128,128]{2,1,0:T(8,128)(2,1)}, u32[]{:S(2)}, u32[]{:S(2)}) collective-permute-start(bf16[28,128,128]{2,1,0:T(8,128)(2,1)} %collective-permute-done.9.refs_5_), channel_id=1, source_target_pairs={{0,2},{1,3},{4,6},{5,7},{8,10},{9,11},{12,14},{13,15},{16,18},{17,... | collective-permute-start | bytes 2752520 | tf_op jit(solution)/shard_map/cond/branch_1_fun/ppermute | solution.py:30
  41.2 27.8 %copy-start.1 = (bf16[44,128,128]{2,1,0:T(8,128)(2,1)}, bf16[44,128,128]{2,1,0:T(8,128)(2,1)S(1)}, u32[]{:S(2)}) copy-start(bf16[44,128,128]{2,1,0:T(8,128)(2,1)S(1)} %collective-permute-done.11.refs_7_) | copy-start | bytes 4325380 | tf_op jit(solution)/shard_map/cond
  41.2 42.6 %collective-permute-start.18 = (bf16[44,128,128]{2,1,0:T(8,128)(2,1)S(1)}, bf16[44,128,128]{2,1,0:T(8,128)(2,1)}, u32[]{:S(2)}, u32[]{:S(2)}) collective-permute-start(bf16[44,128,128]{2,1,0:T(8,128)(2,1)S(1)} %collective-permute-done.11.refs_7_), channel_id=1, source_target_pairs={{3,0},{7,4},{11,8},{15,12},{19,16},{23,20},{27,24},{31,28}} | collective-permute-start | bytes 4325384 | tf_op jit(solution)/shard_map/cond/branch_1_fun/ppermute | solution.py:30
  45.3 31.5 %collective-permute-start.16 = (bf16[40,128,128]{2,1,0:T(8,128)(2,1)}, bf16[40,128,128]{2,1,0:T(8,128)(2,1)}, u32[]{:S(2)}, u32[]{:S(2)}) collective-permute-start(bf16[40,128,128]{2,1,0:T(8,128)(2,1)} %collective-permute-done.10.refs_6_), channel_id=1, source_target_pairs={{0,4},{1,5},{4,8},{5,9},{8,12},{9,13},{16,20},{17,21},{20,24},{21,... | collective-permute-start | bytes 3932168 | tf_op jit(solution)/shard_map/cond/branch_1_fun/ppermute | solution.py:30
  46.6 26.9 %collective-permute-start.17 = (bf16[30,128,128]{2,1,0:T(8,128)(2,1)}, bf16[30,128,128]{2,1,0:T(8,128)(2,1)}, u32[]{:S(2)}, u32[]{:S(2)}) collective-permute-start(bf16[30,128,128]{2,1,0:T(8,128)(2,1)} %collective-permute-done.12.refs_8_), channel_id=1, source_target_pairs={{1,0},{2,1},{5,4},{6,5},{9,8},{10,9},{13,12},{14,13},{17,16},{18,1... | collective-permute-start | bytes 2949128 | tf_op jit(solution)/shard_map/cond/branch_1_fun/ppermute | solution.py:30
  52.5 20.5 %collective-permute-start.15 = (bf16[28,128,128]{2,1,0:T(8,128)(2,1)}, bf16[28,128,128]{2,1,0:T(8,128)(2,1)}, u32[]{:S(2)}, u32[]{:S(2)}) collective-permute-start(bf16[28,128,128]{2,1,0:T(8,128)(2,1)} %collective-permute-done.9.refs_5_), channel_id=1, source_target_pairs={{2,6},{6,10},{10,14},{18,22},{22,26},{26,30}} | collective-permute-start | bytes 2752520 | tf_op jit(solution)/shard_map/cond/branch_1_fun/ppermute | solution.py:30
  64.0 19.0 %collective-permute-start.19 = (bf16[20,128,128]{2,1,0:T(8,128)(2,1)}, bf16[20,128,128]{2,1,0:T(8,128)(2,1)}, u32[]{:S(2)}, u32[]{:S(2)}) collective-permute-start(bf16[20,128,128]{2,1,0:T(8,128)(2,1)} %collective-permute-done.13.refs_9_), channel_id=1, source_target_pairs={{0,2},{4,6},{8,10},{12,14},{16,18},{20,22},{24,26},{28,30}} | collective-permute-start | bytes 1966088 | tf_op jit(solution)/shard_map/cond/branch_1_fun/ppermute | solution.py:30
  89.2 2.3 %collective-permute-start.21 = (f32[8,64]{1,0:T(8,128)S(1)}, f32[8,64]{1,0:T(8,128)S(1)}, u32[]{:S(2)}, u32[]{:S(2)}) collective-permute-start(f32[8,64]{1,0:T(8,128)S(1)} %constant_dynamic-slice_fusion), channel_id=1, source_target_pairs={{0,16},{16,0},{1,17},{17,1},{2,18},{18,2},{3,19},{19,3},{4,20},{20... | collective-permute-start | bytes 6152 | tf_op jit(solution)/shard_map/ppermute | solution.py:24
where the time goes:
time: 92.8 us; the launch traced here: 92.2 us
  waiting for transfers between devices  32.6 us (35%)
  Pallas kernels  29.8 us (32%)
  starting transfers between devices  20.5 us (22%)
  local copies, waits for them, and re-layouts  3.76 us (4%)
  other arithmetic  3.17 us (3%)
  matrix products  1.21 us (1%)
    ppermute x11, waiting for transfers between devices, moved(): return lax.ppermute(x, 'row', [(i, j) for i, j in route if j < size])  31.8 us
    pallas_call x4, Pallas kernels, count_tiles(): pl.pallas_call(lambda *refs: count_kernel(groups, rows, *refs), out_shape...  21.5 us
    ppermute x11, starting transfers between devices, moved(): return lax.ppermute(x, 'row', [(i, j) for i, j in route if j < size])  18.4 us
    pallas_call x1, Pallas kernels, gather_tiles(): pl.pallas_call(lambda *refs: gather_kernel(pieces, *refs), out_shape=[jax...  5.52 us
    pallas_call x1, Pallas kernels, work_list(): pl.pallas_call(lambda *refs: list_kernel(cut, half, *refs), out_shape=[ja...  2.79 us
    ppermute x2, starting transfers between devices, swap_cores(): return lax.ppermute(x, 'rep', [(0, 1), (1, 0)])  2.14 us
    another operation x3, local copies, waits for them, and re-layouts  1.99 us
  transfers between devices with their start and end apart: 13, of which 8 were waited for; matrix products, arithmetic and copies ran while one was open for 6% of the time, Pallas kernels for 20%

commit v1 on v0

--- a/solution.py
+++ b/solution.py
@@ -1,5 +1,6 @@
 import jax
 import jax.numpy as jnp
+import numpy as np
 from jax import lax
 from jax.experimental import pallas as pl
 from jax.experimental.pallas import tpu as pltpu
@@ -8,15 +9,15 @@
 
 BACK = 4
 UNROLL = 8
-(OWN, SIDE0, SIDE1, NEXT, UP3, UP) = range(6)
-(SIDE_NEXT0, SIDE_NEXT1, SIDE_UP, NEXT_UP, UP3_DIAG, UP_DOWN) = range(6, 12)
-GROUPS = 12
-SPLIT = (SIDE0, SIDE_NEXT0)
+(OWN, SIDE0, SIDE1, NEXT, UP3A, UP3B, UP) = range(7)
+(SIDE_NEXT0, SIDE_NEXT1, SIDE_UP, NEXT_UP, DIAGA, DIAGB, UP_DOWN) = range(7, 14)
+GROUPS = 14
+SPLIT = (SIDE0, SIDE_NEXT0, UP3A, DIAGA)
 ARRIVES = (
-    (UP3_DIAG, NEXT_UP, UP_DOWN, UP),
+    (DIAGA, NEXT_UP, UP_DOWN, UP),
     (SIDE0, NEXT_UP, UP_DOWN, UP),
     (SIDE_NEXT0, NEXT, SIDE_UP, UP),
-    (SIDE0, NEXT, SIDE_NEXT0, UP3),
+    (SIDE0, NEXT, SIDE_NEXT0, UP3A),
 )
 
 
@@ -172,7 +173,7 @@
     )(starts, items, before, mine, other, *bufs)
 
 
-def list_kernel(cut, half, near_ref, spot_ref, row_ref, column_ref, group_ref, a_ref, b_ref, start_ref, item_ref):
+def list_kernel(cuts, half, near_ref, spot_ref, row_ref, column_ref, group_ref, a_ref, b_ref, start_ref, item_ref):
     slots, lanes = near_ref.shape
     f32, bf16 = jnp.float32, jnp.bfloat16
     down = lax.broadcasted_iota(jnp.int32, (lanes, lanes), 0)
@@ -192,6 +193,7 @@
 
     group = jnp.broadcast_to(group_ref[...], found.shape)
     for split in SPLIT:
+        cut = cuts[split in (UP3A, DIAGA)]
         second = (group_ref[...] == split) & (found > cut)
         group = jnp.where(second, split + 1, group)
         found = jnp.where(second, found - cut, found)
@@ -279,13 +281,13 @@
     )
 
 
-def work_list(inputs, cut, rows, half):
+def work_list(inputs, cuts, rows, half):
     slots, lanes = inputs[0].shape
     limit = rows * slots * (slots + 1) // 2 + GROUPS * UNROLL
     depth = -(-limit // (8 * lanes)) * 8
     vmem = pl.BlockSpec(memory_space=pltpu.VMEM)
     return pl.pallas_call(
-        lambda *refs: list_kernel(cut, half, *refs),
+        lambda *refs: list_kernel(cuts, half, *refs),
         out_shape=[
             jax.ShapeDtypeStruct((8, lanes), jnp.int32),
             jax.ShapeDtypeStruct((depth, lanes), jnp.int32),
@@ -320,34 +322,35 @@
     index = jnp.sum(jnp.where(match, loc, 0), axis=2)
 
     def run(caps):
-        cut, rest = caps[0], caps[1]
+        (side_a, side_b), next_cap, (up3_a, up3_b), up_cap = caps
 
         def exchange(mine, other, index, inputs):
-            pieces = [(0, 0, cut), (1, 0, caps[2]), (2, 0, caps[3]), (2, 0, caps[4])]
-            pieces += [(0, cut, rest)] * (rest > 0)
+            pieces = [(0, 0, side_a), (2, 0, up3_a), (1, 0, next_cap)]
+            pieces += [(0, side_a, side_b), (2, up3_a, up3_b)] * (side_b > 0)
+            pieces += [(2, 0, up_cap)]
             sent = gather_tiles(pieces, index, mine, other)
-            sent, inputs = lax.optimization_barrier((sent, inputs))
-            pair = {0: 1, 1: -1, 2: 1, 3: -1}
-            side0 = moved(sent[0], pair)
-            up3 = moved(sent[2], {3: 4})
-            second = moved(sent[1], {0: 2, 1: 2, 2: -2, 3: -2})
-            up = moved(sent[3], {0: 4, 1: 4, 2: 4})
-            side1 = moved(sent[4], pair) if rest else None
-            starts, items = work_list(inputs, cut, rows, half)
+            sent, group = lax.optimization_barrier((sent, inputs[4]))
+            inputs = inputs[:4] + (group,) + inputs[5:]
+            early, middle, late = {}, {}, {}
+            early[SIDE0] = side0 = moved(sent[0], {0: 1, 1: -1, 2: 1, 3: -1})
+            early[UP3A] = moved(sent[1], {3: 4})
+            early[NEXT] = moved(sent[2], {0: 2, 1: 2, 2: -2, 3: -2})
+            if side_b:
+                early[SIDE1] = moved(sent[3], {0: 1, 1: -1, 2: 1})
+                early[UP3B] = moved(sent[4], {3: 4})
+            early[UP] = moved(sent[-1], {0: 4, 1: 4, 2: 4})
+            starts, items = work_list(inputs, (side_a, up3_a), rows, half)
             counts = jnp.zeros((rows, tile), jnp.float32)
             counts = count_tiles((), rows, starts, items, counts, mine, other, [], 10**9)
-            side0, counts = lax.optimization_barrier((side0, counts))
-            side_next0 = moved(side0, {0: 2, 1: 2})
-            side_up = moved(side0, {2: 4})
-            up_down = moved(up, {1: -1, 2: -1})
-            next_up = moved(second, {0: 4, 1: 4})
-            up3_diag = moved(up3, {3: -3})
-            early = {SIDE0: side0, NEXT: second, UP3: up3, UP: up}
-            middle = {SIDE_NEXT0: side_next0, SIDE_UP: side_up, NEXT_UP: next_up, UP_DOWN: up_down}
-            late = {UP3_DIAG: up3_diag}
-            if rest:
-                early[SIDE1] = side1
-                late[SIDE_NEXT1] = moved(side1, {0: 2})
+            second, counts = lax.optimization_barrier((early[NEXT], counts))
+            middle[SIDE_NEXT0] = moved(side0, {0: 2, 1: 2})
+            middle[SIDE_UP] = moved(side0, {2: 4})
+            middle[DIAGA] = moved(early[UP3A], {3: -3})
+            late[UP_DOWN] = moved(early[UP], {1: -1, 2: -1})
+            middle[NEXT_UP] = moved(second, {0: 4, 1: 4})
+            if side_b:
+                late[DIAGB] = moved(early[UP3B], {3: -3})
+                late[SIDE_NEXT1] = moved(early[SIDE1], {0: 2})
             for bufs in (early, middle, late):
                 counts = count_tiles(
                     tuple(bufs), rows, starts, items, counts, mine, other, list(bufs.values()), 10**9
@@ -356,18 +359,24 @@
 
         return exchange
 
-    place = jnp.arange(totals.shape[0]) % BACK
-
-    def fit(caps):
-        upper = jnp.where(place == 3, caps[3], caps[4])
-        sizes = jnp.stack([ahead, totals[:, 0], totals[:, 1], totals[:, 2]], axis=1)
-        bound = [jnp.full_like(place, c) for c in (caps[0], caps[0] + caps[1], caps[2])] + [upper]
-        return jnp.all(sizes <= 2 * jnp.stack(bound, axis=1))
-
-    brief = (full * 7 // 16, full * 5 // 16, full * 5 // 8, full * 11 // 16, full * 15 // 32)
-    most = (full, 0, full, full, full)
+    unit = full // 32
+    tiers = (
+        ((12 * unit, 12 * unit), 17 * unit, (11 * unit, 10 * unit), 13 * unit),
+        ((13 * unit, 12 * unit), 19 * unit, (12 * unit, 10 * unit), 15 * unit),
+        ((14 * unit, 14 * unit), 23 * unit, (13 * unit, 12 * unit), 20 * unit),
+        ((full, 0), full, (full, 0), full),
+    )
+    bounds = np.zeros((len(tiers) - 1, BACK, 4), np.int32)
+    for bound, (side, second, up3, up) in zip(bounds, tiers):
+        for at in range(BACK):
+            upper = sum(up3) if at == BACK - 1 else up
+            bound[at] = (2 * side[0], 2 * sum(side), 2 * second, 2 * upper)
+    sizes = jnp.concatenate([ahead[:, None], totals], axis=1).reshape(1, -1, BACK, 4)
+    fits = jnp.all(sizes <= bounds[:, None], axis=(1, 2, 3))
+    choice = len(tiers) - 1 - jnp.sum(fits.astype(jnp.int32))
     inputs = list_inputs(tile_cols, lists, ranks, rows, here, core, loc)
-    partial = lax.cond(fit(brief), run(brief), run(most), mine, other, index, inputs)
+    runs = [run(caps) for caps in tiers]
+    partial = lax.switch(choice, runs, mine, other, index, inputs)
 
     width = tile // 2
     keep = lax.dynamic_slice_in_dim(partial, core * width, width, 1)

time: 92.8 us -> 99.1 us (1.068)
  starting transfers between devices: 20.5 us -> 29.1 us
  waiting for transfers between devices: 32.6 us -> 27.9 us
  local copies, waits for them, and re-layouts: 3.76 us -> 4.99 us
  other arithmetic: 3.17 us -> 4.34 us
    ppermute x11 -> x13, starting transfers between devices: 18.4 us -> 26 us  [moved(): return lax.ppermute(x, 'row', [(i, j) for i, j in route if j < size])]
    ppermute x11 -> x13, waiting for transfers between devices: 31.8 us -> 27.1 us  [moved(): return lax.ppermute(x, 'row', [(i, j) for i, j in route if j < size])]
    ppermute x2, starting transfers between devices: 2.14 us -> 3.16 us  [swap_cores(): return lax.ppermute(x, 'rep', [(0, 1), (1, 0)])]
  transfers between devices with their start and end apart: 13 -> 15, of which waited for: 8 -> 4; matrix products, arithmetic and copies ran while one was open for 6% -> 9% of each run, Pallas kernels for 20% -> 20%
where the time goes in v1:
time: 99.1 us; the launch traced here: 98.3 us
  Pallas kernels  29.4 us (30%)
  starting transfers between devices  29.1 us (29%)
  waiting for transfers between devices  27.9 us (28%)
  local copies, waits for them, and re-layouts  4.99 us (5%)
  other arithmetic  4.34 us (4%)
  matrix products  1.21 us (1%)
    ppermute x13, waiting for transfers between devices, moved(): return lax.ppermute(x, 'row', [(i, j) for i, j in route if j < size])  27.1 us
    ppermute x13, starting transfers between devices, moved(): return lax.ppermute(x, 'row', [(i, j) for i, j in route if j < size])  26 us
    pallas_call x4, Pallas kernels, count_tiles(): pl.pallas_call(lambda *refs: count_kernel(groups, rows, *refs), out_shape...  21.3 us
    pallas_call x1, Pallas kernels, gather_tiles(): pl.pallas_call(lambda *refs: gather_kernel(pieces, *refs), out_shape=[jax...  5.36 us
    ppermute x2, starting transfers between devices, swap_cores(): return lax.ppermute(x, 'rep', [(0, 1), (1, 0)])  3.16 us
    pallas_call x1, Pallas kernels, work_list(): pl.pallas_call(lambda *refs: list_kernel(cuts, half, *refs), out_shape=[j...  2.79 us
    another operation x3, local copies, waits for them, and re-layouts  1.99 us
  transfers between devices with their start and end apart: 15, of which 4 were waited for; matrix products, arithmetic and copies ran while one was open for 9% of the time, Pallas kernels for 20%

profile of v1, /device:TPU:25, one launch (start us, length us, event | category | flops | bytes accessed | tf_op | source)
XLA Modules:
  0.0 98.3 jit_solution(7953953036711919344)
XLA Ops:
  8.4 85.9 %conditional.1 = (f32[8,128]{1,0:T(8,128)S(1)}) conditional(s32[]{:T(128)} %clamp.3, (s32[3,64]{1,0:T(4,128)S(1)}, bf16[64,128,128]{2,1,0:T(8,128)(2,1)S(1)}, bf16[64,128,128]{2,1,0:T(8,128)(2,1)}, s32[1,128]{1,0:T(1,128)S(1)}, s32[16,128]{1,0:T(8,128)S(1)}, /*index=5*/s32[16,128]{0,1:T(8,128)S(1)}, ...), branch_computations={%region_9.10_spmd, %region_10.11_spmd, %region_11.12_spmd, %region... | conditional | flops 5000999936 | bytes 124396568 | solution.py:379
  8.5 5.4 %branch_0_fun.6 = (bf16[24,128,128]{2,1,0:T(8,128)(2,1)}, bf16[22,128,128]{2,1,0:T(8,128)(2,1)}, bf16[34,128,128]{2,1,0:T(8,128)(2,1)}, bf16[24,128,128]{2,1,0:T...) custom-call(s32[3,64]{1,0:T(4,128)S(1)} %get-tuple-element.94.refs_0_, ...), custom_call_target="tpu_custom_call" | custom-call | flops 1000000 | bytes 9830400 | tf_op jit(solution)/shard_map/cond/branch_0_fun/pallas_call | solution.py:94
  13.8 1.3 %collective-permute-start = (bf16[34,128,128]{2,1,0:T(8,128)(2,1)}, bf16[34,128,128]{2,1,0:T(8,128)(2,1)}, u32[]{:S(2)}, u32[]{:S(2)}) collective-permute-start(bf16[34,128,128]{2,1,0:T(8,128)(2,1)} %get-tuple-element.109), channel_id=1, source_target_pairs={{0,2},{1,3},{2,0},{3,1},{4,6},{5,7},{6,4},{7,5},{8,10},{9,11},{10,... | collective-permute-start | bytes 3342344 | tf_op jit(solution)/shard_map/cond/branch_0_fun/ppermute | solution.py:31
  15.1 1.5 %collective-permute-start.2 = (bf16[22,128,128]{2,1,0:T(8,128)(2,1)}, bf16[22,128,128]{2,1,0:T(8,128)(2,1)}, u32[]{:S(2)}, u32[]{:S(2)}) collective-permute-start(bf16[22,128,128]{2,1,0:T(8,128)(2,1)} %get-tuple-element.112), channel_id=1, source_target_pairs={{3,7},{7,11},{11,15},{19,23},{23,27},{27,31}} | collective-permute-start | bytes 2162696 | tf_op jit(solution)/shard_map/cond/branch_0_fun/ppermute | solution.py:31
  16.7 1.2 %collective-permute-start.1 = (bf16[24,128,128]{2,1,0:T(8,128)(2,1)}, bf16[24,128,128]{2,1,0:T(8,128)(2,1)}, u32[]{:S(2)}, u32[]{:S(2)}) collective-permute-start(bf16[24,128,128]{2,1,0:T(8,128)(2,1)} %get-tuple-element.111), channel_id=1, source_target_pairs={{0,1},{1,0},{2,3},{3,2},{4,5},{5,4},{6,7},{7,6},{8,9},{9,8},{10,11... | collective-permute-start | bytes 2359304 | tf_op jit(solution)/shard_map/cond/branch_0_fun/ppermute | solution.py:31
  17.9 1.5 %collective-permute-start.4 = (bf16[20,128,128]{2,1,0:T(8,128)(2,1)}, bf16[20,128,128]{2,1,0:T(8,128)(2,1)}, u32[]{:S(2)}, u32[]{:S(2)}) collective-permute-start(bf16[20,128,128]{2,1,0:T(8,128)(2,1)} %get-tuple-element.114), channel_id=1, source_target_pairs={{3,7},{7,11},{11,15},{19,23},{23,27},{27,31}} | collective-permute-start | bytes 1966088 | tf_op jit(solution)/shard_map/cond/branch_0_fun/ppermute | solution.py:31
  19.3 1.3 %collective-permute-start.5 = (bf16[26,128,128]{2,1,0:T(8,128)(2,1)}, bf16[26,128,128]{2,1,0:T(8,128)(2,1)}, u32[]{:S(2)}, u32[]{:S(2)}) collective-permute-start(bf16[26,128,128]{2,1,0:T(8,128)(2,1)} %get-tuple-element.115), channel_id=1, source_target_pairs={{0,4},{1,5},{2,6},{4,8},{5,9},{6,10},{8,12},{9,13},{10,14},{16,20}... | collective-permute-start | bytes 2555912 | tf_op jit(solution)/shard_map/cond/branch_0_fun/ppermute | solution.py:31
  20.6 2.2 %collective-permute-start.3 = (bf16[24,128,128]{2,1,0:T(8,128)(2,1)}, bf16[24,128,128]{2,1,0:T(8,128)(2,1)}, u32[]{:S(2)}, u32[]{:S(2)}) collective-permute-start(bf16[24,128,128]{2,1,0:T(8,128)(2,1)} %get-tuple-element.113), channel_id=1, source_target_pairs={{0,1},{1,0},{2,3},{4,5},{5,4},{6,7},{8,9},{9,8},{10,11},{12,13},{1... | collective-permute-start | bytes 2359304 | tf_op jit(solution)/shard_map/cond/branch_0_fun/ppermute | solution.py:31
  22.8 12.8 %collective-permute-done.1.refs_5_ = bf16[24,128,128]{2,1,0:T(8,128)(2,1)} collective-permute-done((bf16[24,128,128]{2,1,0:T(8,128)(2,1)}, bf16[24,128,128]{2,1,0:T(8,128)(2,1)}, u32[]{:S(2)}, u32[]{:S(2)}) %collective-permute-start.1) | collective-permute-done | bytes 786464 | tf_op jit(solution)/shard_map/cond/branch_0_fun/ppermute | solution.py:31
  35.6 1.3 %collective-permute-start.8 = (bf16[22,128,128]{2,1,0:T(8,128)(2,1)}, bf16[22,128,128]{2,1,0:T(8,128)(2,1)}, u32[]{:S(2)}, u32[]{:S(2)}) collective-permute-start(bf16[22,128,128]{2,1,0:T(8,128)(2,1)} %collective-permute-done.2.refs_6_), channel_id=1, source_target_pairs={{3,0},{7,4},{11,8},{15,12},{19,16},{23,20},{27,24},{31,28}} | collective-permute-start | bytes 2162696 | tf_op jit(solution)/shard_map/cond/branch_0_fun/ppermute | solution.py:31
  36.9 3.3 %collective-permute-done.refs_7_ = bf16[34,128,128]{2,1,0:T(8,128)(2,1)} collective-permute-done((bf16[34,128,128]{2,1,0:T(8,128)(2,1)}, bf16[34,128,128]{2,1,0:T(8,128)(2,1)}, u32[]{:S(2)}, u32[]{:S(2)}) %collective-permute-start) | collective-permute-done | bytes 1114144 | tf_op jit(solution)/shard_map/cond/branch_0_fun/ppermute | solution.py:31
  40.2 4.1 %collective-permute-start.6 = (bf16[24,128,128]{2,1,0:T(8,128)(2,1)}, bf16[24,128,128]{2,1,0:T(8,128)(2,1)}, u32[]{:S(2)}, u32[]{:S(2)}) collective-permute-start(bf16[24,128,128]{2,1,0:T(8,128)(2,1)} %collective-permute-done.1.refs_5_), channel_id=1, source_target_pairs={{0,2},{1,3},{4,6},{5,7},{8,10},{9,11},{12,14},{13,15},{16,18},{17,... | collective-permute-start | bytes 2359304 | tf_op jit(solution)/shard_map/cond/branch_0_fun/ppermute | solution.py:31
  45.7 2.8 %branch_0_fun.7 = (s32[8,128]{1,0:T(8,128)}, s32[16,128]{1,0:T(8,128)}) custom-call(s32[16,128]{1,0:T(8,128)S(1)} %get-tuple-element.88.refs_0_, s32[16,128]{1,0:T(8,128)} %copy.103.refs_1_, s32[1,128]{1,0:T(1,128)S(1)} %get-tuple-element.92.refs_2_, s32[128,1]{1,0:T(8,128)} %copy.104.refs_3_, s32[1,128]{1,0:T(1,128)S(1)} %get-tuple-element.104.refs_4_, ...), custom_call_target="tpu_custom_call" | custom-call | flops 1000000000 | bytes 100000 | tf_op jit(solution)/shard_map/cond/branch_0_fun/pallas_call | solution.py:289
  49.0 6.0 %branch_0_fun.8.refs_2_ = f32[8,128]{1,0:T(8,128)} custom-call(s32[8,128]{1,0:T(8,128)} %get-tuple-element.107.refs_0_, s32[16,128]{1,0:T(8,128)} %get-tuple-element.108.refs_1_, f32[8,128]{1,0:T(8,128)} %broadcast_21_refs_2_.0.refs_2_, bf16[64,128,128]{2,1,0:T(8,128)(2,1)S(1)} %get-tuple-element.95.refs_1_.refs_3_, ...), custom_call_target="tpu_custom_call" | custom-call | flops 1000000000 | bytes 8000000 | tf_op jit(solution)/shard_map/cond/branch_0_fun/pallas_call | solution.py:161
  55.1 1.3 %collective-permute-start.9 = (bf16[34,128,128]{2,1,0:T(8,128)(2,1)}, bf16[34,128,128]{2,1,0:T(8,128)(2,1)S(1)}, u32[]{:S(2)}, u32[]{:S(2)}) collective-permute-start(bf16[34,128,128]{2,1,0:T(8,128)(2,1)} %collective-permute-done.refs_7_), channel_id=1, source_target_pairs={{0,4},{1,5},{4,8},{5,9},{8,12},{9,13},{16,20},{17,21},{20,24},{21,... | collective-permute-start | bytes 3342344 | tf_op jit(solution)/shard_map/cond/branch_0_fun/ppermute | solution.py:31
  56.4 1.6 %collective-permute-start.7 = (bf16[24,128,128]{2,1,0:T(8,128)(2,1)}, bf16[24,128,128]{2,1,0:T(8,128)(2,1)}, u32[]{:S(2)}, u32[]{:S(2)}) collective-permute-start(bf16[24,128,128]{2,1,0:T(8,128)(2,1)} %collective-permute-done.1.refs_5_), channel_id=1, source_target_pairs={{2,6},{6,10},{10,14},{18,22},{22,26},{26,30}} | collective-permute-start | bytes 2359304 | tf_op jit(solution)/shard_map/cond/branch_0_fun/ppermute | solution.py:31
  57.9 1.3 %collective-permute-start.10 = (bf16[26,128,128]{2,1,0:T(8,128)(2,1)}, bf16[26,128,128]{2,1,0:T(8,128)(2,1)}, u32[]{:S(2)}, u32[]{:S(2)}) collective-permute-start(bf16[26,128,128]{2,1,0:T(8,128)(2,1)} %collective-permute-done.5.refs_10_), channel_id=1, source_target_pairs={{1,0},{2,1},{5,4},{6,5},{9,8},{10,9},{13,12},{14,13},{17,16},{18,1... | collective-permute-start | bytes 2555912 | tf_op jit(solution)/shard_map/cond/branch_0_fun/ppermute | solution.py:31
  59.2 6.3 %collective-permute-start.12 = (bf16[24,128,128]{2,1,0:T(8,128)(2,1)}, bf16[24,128,128]{2,1,0:T(8,128)(2,1)}, u32[]{:S(2)}, u32[]{:S(2)}) collective-permute-start(bf16[24,128,128]{2,1,0:T(8,128)(2,1)} %collective-permute-done.3.refs_8_), channel_id=1, source_target_pairs={{0,2},{4,6},{8,10},{12,14},{16,18},{20,22},{24,26},{28,30}} | collective-permute-start | bytes 2359304 | tf_op jit(solution)/shard_map/cond/branch_0_fun/ppermute | solution.py:31
  65.5 1.3 %collective-permute-start.11 = (bf16[20,128,128]{2,1,0:T(8,128)(2,1)}, bf16[20,128,128]{2,1,0:T(8,128)(2,1)}, u32[]{:S(2)}, u32[]{:S(2)}) collective-permute-start(bf16[20,128,128]{2,1,0:T(8,128)(2,1)} %collective-permute-done.4.refs_9_), channel_id=1, source_target_pairs={{3,0},{7,4},{11,8},{15,12},{19,16},{23,20},{27,24},{31,28}} | collective-permute-start | bytes 1966088 | tf_op jit(solution)/shard_map/cond/branch_0_fun/ppermute | solution.py:31
  66.8 3.9 %branch_0_fun.9.refs_2_ = f32[8,128]{1,0:T(8,128)} custom-call(s32[8,128]{1,0:T(8,128)} %get-tuple-element.107.refs_0_, s32[16,128]{1,0:T(8,128)} %get-tuple-element.108.refs_1_, f32[8,128]{1,0:T(8,128)} %branch_0_fun.8.refs_2_, bf16[64,128,128]{2,1,0:T(8,128)(2,1)S(1)} %get-tuple-element.95.refs_1_.refs_3_, ...), custom_call_target="tpu_custom_call" | custom-call | flops 1000000000 | bytes 8000000 | tf_op jit(solution)/shard_map/cond/branch_0_fun/pallas_call | solution.py:161
  70.7 11.0 %collective-permute-done.9.refs_8_ = bf16[34,128,128]{2,1,0:T(8,128)(2,1)S(1)} collective-permute-done((bf16[34,128,128]{2,1,0:T(8,128)(2,1)}, bf16[34,128,128]{2,1,0:T(8,128)(2,1)S(1)}, u32[]{:S(2)}, u32[]{:S(2)}) %collective-permute-start.9) | collective-permute-done | bytes 1114144 | tf_op jit(solution)/shard_map/cond/branch_0_fun/ppermute | solution.py:31
  82.7 6.7 %branch_0_fun.10.refs_2_ = f32[8,128]{1,0:T(8,128)} custom-call(s32[8,128]{1,0:T(8,128)} %get-tuple-element.107.refs_0_, s32[16,128]{1,0:T(8,128)} %get-tuple-element.108.refs_1_, f32[8,128]{1,0:T(8,128)} %branch_0_fun.9.refs_2_, bf16[64,128,128]{2,1,0:T(8,128)(2,1)S(1)} %get-tuple-element.95.refs_1_.refs_3_, ...), custom_call_target="tpu_custom_call" | custom-call | flops 1000000000 | bytes 8000000 | tf_op jit(solution)/shard_map/cond/branch_0_fun/pallas_call | solution.py:161
  89.4 4.7 %branch_0_fun.11 = f32[8,128]{1,0:T(8,128)S(1)} custom-call(s32[8,128]{1,0:T(8,128)} %get-tuple-element.107.refs_0_, s32[16,128]{1,0:T(8,128)} %get-tuple-element.108.refs_1_, f32[8,128]{1,0:T(8,128)} %branch_0_fun.10.refs_2_, bf16[64,128,128]{2,1,0:T(8,128)(2,1)S(1)} %get-tuple-element.95.refs_1_.refs_3_, ...), custom_call_target="tpu_custom_call" | custom-call | flops 1000000000 | bytes 8000000 | tf_op jit(solution)/shard_map/cond/branch_0_fun/pallas_call | solution.py:161
  94.4 2.4 %collective-permute-start.49 = (f32[8,64]{1,0:T(8,128)S(1)}, f32[8,64]{1,0:T(8,128)S(1)}, u32[]{:S(2)}, u32[]{:S(2)}) collective-permute-start(f32[8,64]{1,0:T(8,128)S(1)} %constant_dynamic-slice_fusion), channel_id=1, source_target_pairs={{0,16},{16,0},{1,17},{17,1},{2,18},{18,2},{3,19},{19,3},{4,20},{20... | collective-permute-start | bytes 6152 | tf_op jit(solution)/shard_map/ppermute | solution.py:25
  (79 shorter events, 12.1 us)
Async XLA Ops:
  0.0 6.6 %copy-start.6 = (s32[3,4,4]{2,1,0:T(4,128)S(1)}, s32[3,4,4]{2,1,0:T(4,128)}, u32[]{:S(2)}) copy-start(s32[3,4,4]{2,1,0:T(4,128)} %constant.235) | copy-start | bytes 580
  0.0 8.4 %copy-start = (bf16[8,8,128,128]{3,2,1,0:T(8,128)(2,1)S(1)}, bf16[8,8,128,128]{3,2,1,0:T(8,128)(2,1)}, u32[]{:S(2)}) copy-start(bf16[8,8,128,128]{3,2,1,0:T(8,128)(2,1)} %param.7) | copy-start | bytes 6291460
  0.0 8.0 %copy-start.5 = (s32[128,16]{0,1:T(8,128)S(1)}, s32[128,16]{0,1:T(8,128)}, u32[]{:S(2)}) copy-start(s32[128,16]{0,1:T(8,128)} %param.8) | copy-start | bytes 24580
  0.0 8.4 %collective-permute-start.48 = (bf16[64,128,128]{2,1,0:T(8,128)(2,1)}, bf16[64,128,128]{2,1,0:T(8,128)(2,1)}, u32[]{:S(2)}, u32[]{:S(2)}) collective-permute-start(bf16[64,128,128]{2,1,0:T(8,128)(2,1)} %bitcast.37), channel_id=1, source_target_pairs={{0,16},{16,0},{1,17},{17,1},{2,18},{18,2},{3,19},{19,3},{4,20},{20... | collective-permute-start | bytes 6291464 | tf_op jit(solution)/shard_map/ppermute | solution.py:25
  13.8 26.4 %collective-permute-start = (bf16[34,128,128]{2,1,0:T(8,128)(2,1)}, bf16[34,128,128]{2,1,0:T(8,128)(2,1)}, u32[]{:S(2)}, u32[]{:S(2)}) collective-permute-start(bf16[34,128,128]{2,1,0:T(8,128)(2,1)} %get-tuple-element.109), channel_id=1, source_target_pairs={{0,2},{1,3},{2,0},{3,1},{4,6},{5,7},{6,4},{7,5},{8,10},{9,11},{10,... | collective-permute-start | bytes 3342344 | tf_op jit(solution)/shard_map/cond/branch_0_fun/ppermute | solution.py:31
  15.1 5.5 %collective-permute-start.2 = (bf16[22,128,128]{2,1,0:T(8,128)(2,1)}, bf16[22,128,128]{2,1,0:T(8,128)(2,1)}, u32[]{:S(2)}, u32[]{:S(2)}) collective-permute-start(bf16[22,128,128]{2,1,0:T(8,128)(2,1)} %get-tuple-element.112), channel_id=1, source_target_pairs={{3,7},{7,11},{11,15},{19,23},{23,27},{27,31}} | collective-permute-start | bytes 2162696 | tf_op jit(solution)/shard_map/cond/branch_0_fun/ppermute | solution.py:31
  16.7 19.0 %collective-permute-start.1 = (bf16[24,128,128]{2,1,0:T(8,128)(2,1)}, bf16[24,128,128]{2,1,0:T(8,128)(2,1)}, u32[]{:S(2)}, u32[]{:S(2)}) collective-permute-start(bf16[24,128,128]{2,1,0:T(8,128)(2,1)} %get-tuple-element.111), channel_id=1, source_target_pairs={{0,1},{1,0},{2,3},{3,2},{4,5},{5,4},{6,7},{7,6},{8,9},{9,8},{10,11... | collective-permute-start | bytes 2359304 | tf_op jit(solution)/shard_map/cond/branch_0_fun/ppermute | solution.py:31
  17.9 37.2 %collective-permute-start.4 = (bf16[20,128,128]{2,1,0:T(8,128)(2,1)}, bf16[20,128,128]{2,1,0:T(8,128)(2,1)}, u32[]{:S(2)}, u32[]{:S(2)}) collective-permute-start(bf16[20,128,128]{2,1,0:T(8,128)(2,1)} %get-tuple-element.114), channel_id=1, source_target_pairs={{3,7},{7,11},{11,15},{19,23},{23,27},{27,31}} | collective-permute-start | bytes 1966088 | tf_op jit(solution)/shard_map/cond/branch_0_fun/ppermute | solution.py:31
  19.3 38.6 %collective-permute-start.5 = (bf16[26,128,128]{2,1,0:T(8,128)(2,1)}, bf16[26,128,128]{2,1,0:T(8,128)(2,1)}, u32[]{:S(2)}, u32[]{:S(2)}) collective-permute-start(bf16[26,128,128]{2,1,0:T(8,128)(2,1)} %get-tuple-element.115), channel_id=1, source_target_pairs={{0,4},{1,5},{2,6},{4,8},{5,9},{6,10},{8,12},{9,13},{10,14},{16,20}... | collective-permute-start | bytes 2555912 | tf_op jit(solution)/shard_map/cond/branch_0_fun/ppermute | solution.py:31
  20.6 35.7 %collective-permute-start.3 = (bf16[24,128,128]{2,1,0:T(8,128)(2,1)}, bf16[24,128,128]{2,1,0:T(8,128)(2,1)}, u32[]{:S(2)}, u32[]{:S(2)}) collective-permute-start(bf16[24,128,128]{2,1,0:T(8,128)(2,1)} %get-tuple-element.113), channel_id=1, source_target_pairs={{0,1},{1,0},{2,3},{4,5},{5,4},{6,7},{8,9},{9,8},{10,11},{12,13},{1... | collective-permute-start | bytes 2359304 | tf_op jit(solution)/shard_map/cond/branch_0_fun/ppermute | solution.py:31
  35.6 23.6 %collective-permute-start.8 = (bf16[22,128,128]{2,1,0:T(8,128)(2,1)}, bf16[22,128,128]{2,1,0:T(8,128)(2,1)}, u32[]{:S(2)}, u32[]{:S(2)}) collective-permute-start(bf16[22,128,128]{2,1,0:T(8,128)(2,1)} %collective-permute-done.2.refs_6_), channel_id=1, source_target_pairs={{3,0},{7,4},{11,8},{15,12},{19,16},{23,20},{27,24},{31,28}} | collective-permute-start | bytes 2162696 | tf_op jit(solution)/shard_map/cond/branch_0_fun/ppermute | solution.py:31
  40.2 25.3 %collective-permute-start.6 = (bf16[24,128,128]{2,1,0:T(8,128)(2,1)}, bf16[24,128,128]{2,1,0:T(8,128)(2,1)}, u32[]{:S(2)}, u32[]{:S(2)}) collective-permute-start(bf16[24,128,128]{2,1,0:T(8,128)(2,1)} %collective-permute-done.1.refs_5_), channel_id=1, source_target_pairs={{0,2},{1,3},{4,6},{5,7},{8,10},{9,11},{12,14},{13,15},{16,18},{17,... | collective-permute-start | bytes 2359304 | tf_op jit(solution)/shard_map/cond/branch_0_fun/ppermute | solution.py:31
  55.1 26.7 %collective-permute-start.9 = (bf16[34,128,128]{2,1,0:T(8,128)(2,1)}, bf16[34,128,128]{2,1,0:T(8,128)(2,1)S(1)}, u32[]{:S(2)}, u32[]{:S(2)}) collective-permute-start(bf16[34,128,128]{2,1,0:T(8,128)(2,1)} %collective-permute-done.refs_7_), channel_id=1, source_target_pairs={{0,4},{1,5},{4,8},{5,9},{8,12},{9,13},{16,20},{17,21},{20,24},{21,... | collective-permute-start | bytes 3342344 | tf_op jit(solution)/shard_map/cond/branch_0_fun/ppermute | solution.py:31
  56.4 14.3 %collective-permute-start.7 = (bf16[24,128,128]{2,1,0:T(8,128)(2,1)}, bf16[24,128,128]{2,1,0:T(8,128)(2,1)}, u32[]{:S(2)}, u32[]{:S(2)}) collective-permute-start(bf16[24,128,128]{2,1,0:T(8,128)(2,1)} %collective-permute-done.1.refs_5_), channel_id=1, source_target_pairs={{2,6},{6,10},{10,14},{18,22},{22,26},{26,30}} | collective-permute-start | bytes 2359304 | tf_op jit(solution)/shard_map/cond/branch_0_fun/ppermute | solution.py:31
  57.9 31.5 %collective-permute-start.10 = (bf16[26,128,128]{2,1,0:T(8,128)(2,1)}, bf16[26,128,128]{2,1,0:T(8,128)(2,1)}, u32[]{:S(2)}, u32[]{:S(2)}) collective-permute-start(bf16[26,128,128]{2,1,0:T(8,128)(2,1)} %collective-permute-done.5.refs_10_), channel_id=1, source_target_pairs={{1,0},{2,1},{5,4},{6,5},{9,8},{10,9},{13,12},{14,13},{17,16},{18,1... | collective-permute-start | bytes 2555912 | tf_op jit(solution)/shard_map/cond/branch_0_fun/ppermute | solution.py:31
  59.2 30.2 %collective-permute-start.12 = (bf16[24,128,128]{2,1,0:T(8,128)(2,1)}, bf16[24,128,128]{2,1,0:T(8,128)(2,1)}, u32[]{:S(2)}, u32[]{:S(2)}) collective-permute-start(bf16[24,128,128]{2,1,0:T(8,128)(2,1)} %collective-permute-done.3.refs_8_), channel_id=1, source_target_pairs={{0,2},{4,6},{8,10},{12,14},{16,18},{20,22},{24,26},{28,30}} | collective-permute-start | bytes 2359304 | tf_op jit(solution)/shard_map/cond/branch_0_fun/ppermute | solution.py:31
  65.5 23.9 %collective-permute-start.11 = (bf16[20,128,128]{2,1,0:T(8,128)(2,1)}, bf16[20,128,128]{2,1,0:T(8,128)(2,1)}, u32[]{:S(2)}, u32[]{:S(2)}) collective-permute-start(bf16[20,128,128]{2,1,0:T(8,128)(2,1)} %collective-permute-done.4.refs_9_), channel_id=1, source_target_pairs={{3,0},{7,4},{11,8},{15,12},{19,16},{23,20},{27,24},{31,28}} | collective-permute-start | bytes 1966088 | tf_op jit(solution)/shard_map/cond/branch_0_fun/ppermute | solution.py:31
  81.7 1.0 %copy-start.4 = (bf16[34,128,128]{2,1,0:T(8,128)(2,1)}, bf16[34,128,128]{2,1,0:T(8,128)(2,1)S(1)}, u32[]{:S(2)}) copy-start(bf16[34,128,128]{2,1,0:T(8,128)(2,1)S(1)} %collective-permute-done.9.refs_8_) | copy-start | bytes 3342340 | tf_op jit(solution)/shard_map/cond
  94.4 3.2 %collective-permute-start.49 = (f32[8,64]{1,0:T(8,128)S(1)}, f32[8,64]{1,0:T(8,128)S(1)}, u32[]{:S(2)}, u32[]{:S(2)}) collective-permute-start(f32[8,64]{1,0:T(8,128)S(1)} %constant_dynamic-slice_fusion), channel_id=1, source_target_pairs={{0,16},{16,0},{1,17},{17,1},{2,18},{18,2},{3,19},{19,3},{4,20},{20... | collective-permute-start | bytes 6152 | tf_op jit(solution)/shard_map/ppermute | solution.py:25

commit v2 on v1

--- a/solution.py
+++ b/solution.py
@@ -84,7 +84,7 @@
             out[p] = pool[index_ref[which, start + p]]
             return carry
 
-        lax.fori_loop(0, cap, one, 0, unroll=2)
+        lax.fori_loop(0, cap, one, 0, unroll=4)
 
 
 def gather_tiles(pieces, index, mine, other):
@@ -156,7 +156,7 @@
 
 def count_tiles(groups, rows, starts, items, before, mine, other, bufs, flops):
     half, tile, _ = mine.shape
-    anywhere = pl.BlockSpec(memory_space=pl.ANY)
+    anywhere = pl.BlockSpec(memory_space=pltpu.HBM)
     vmem = pl.BlockSpec(memory_space=pltpu.VMEM)
     return pl.pallas_call(
         lambda *refs: count_kernel(groups, rows, *refs),
@@ -300,7 +300,7 @@
 
 def body(tiles, tile_cols):
     rows, half_slots, tile, _ = tiles.shape
-    _, slots = tile_cols.shape
+    count, slots = tile_cols.shape
     core = lax.axis_index("rep")
     here = lax.axis_index("row")
     half = rows * half_slots
@@ -346,7 +346,7 @@
             middle[SIDE_NEXT0] = moved(side0, {0: 2, 1: 2})
             middle[SIDE_UP] = moved(side0, {2: 4})
             middle[DIAGA] = moved(early[UP3A], {3: -3})
-            late[UP_DOWN] = moved(early[UP], {1: -1, 2: -1})
+            middle[UP_DOWN] = moved(early[UP], {1: -1, 2: -1})
             middle[NEXT_UP] = moved(second, {0: 4, 1: 4})
             if side_b:
                 late[DIAGB] = moved(early[UP3B], {3: -3})
@@ -371,8 +371,9 @@
         for at in range(BACK):
             upper = sum(up3) if at == BACK - 1 else up
             bound[at] = (2 * side[0], 2 * sum(side), 2 * second, 2 * upper)
-    sizes = jnp.concatenate([ahead[:, None], totals], axis=1).reshape(1, -1, BACK, 4)
-    fits = jnp.all(sizes <= bounds[:, None], axis=(1, 2, 3))
+    bounds = np.tile(bounds, (1, count // rows // BACK, 1))
+    sizes = jnp.concatenate([ahead[:, None], totals], axis=1)
+    fits = jnp.all(sizes <= bounds, axis=(1, 2))
     choice = len(tiers) - 1 - jnp.sum(fits.astype(jnp.int32))
     inputs = list_inputs(tile_cols, lists, ranks, rows, here, core, loc)
     runs = [run(caps) for caps in tiers]

time: 99.1 us -> 96.4 us (0.973)
  local copies, waits for them, and re-layouts: 4.99 us -> 3.74 us
  other arithmetic: 4.34 us -> 3.21 us
  transfers between devices with their start and end apart: 15 -> 15, of which waited for: 4 -> 5; matrix products, arithmetic and copies ran while one was open for 9% -> 8% of each run, Pallas kernels for 20% -> 21%
where the time goes in v2:
time: 96.4 us; the launch traced here: 95.6 us
  Pallas kernels  29.2 us (30%)
  starting transfers between devices  29 us (30%)
  waiting for transfers between devices  28 us (29%)
  local copies, waits for them, and re-layouts  3.74 us (4%)
  other arithmetic  3.21 us (3%)
  matrix products  1.21 us (1%)
    ppermute x13, waiting for transfers between devices, moved(): return lax.ppermute(x, 'row', [(i, j) for i, j in route if j < size])  27.1 us
    ppermute x13, starting transfers between devices, moved(): return lax.ppermute(x, 'row', [(i, j) for i, j in route if j < size])  25.8 us
    pallas_call x4, Pallas kernels, count_tiles(): pl.pallas_call(lambda *refs: count_kernel(groups, rows, *refs), out_shape...  21.2 us
    pallas_call x1, Pallas kernels, gather_tiles(): pl.pallas_call(lambda *refs: gather_kernel(pieces, *refs), out_shape=[jax...  5.17 us
    ppermute x2, starting transfers between devices, swap_cores(): return lax.ppermute(x, 'rep', [(0, 1), (1, 0)])  3.27 us
    pallas_call x1, Pallas kernels, work_list(): pl.pallas_call(lambda *refs: list_kernel(cuts, half, *refs), out_shape=[j...  2.79 us
    another operation x3, local copies, waits for them, and re-layouts  1.98 us
  transfers between devices with their start and end apart: 15, of which 5 were waited for; matrix products, arithmetic and copies ran while one was open for 8% of the time, Pallas kernels for 21%

profile of v2, /device:TPU:25, one launch (start us, length us, event | category | flops | bytes accessed | tf_op | source)
XLA Modules:
  0.0 95.6 jit_solution(15023448622411469841)
XLA Ops:
  7.1 84.4 %conditional.1 = (f32[8,128]{1,0:T(8,128)S(1)}) conditional(s32[]{:T(128)} %clamp.3, (s32[3,64]{1,0:T(4,128)S(1)}, bf16[64,128,128]{2,1,0:T(8,128)(2,1)S(1)}, bf16[64,128,128]{2,1,0:T(8,128)(2,1)}, s32[1,128]{1,0:T(1,128)S(1)}, s32[16,128]{1,0:T(8,128)S(1)}, /*index=5*/s32[16,128]{0,1:T(8,128)S(1)}, ...), branch_computations={%region_9.10_spmd, %region_10.11_spmd, %region_11.12_spmd, %region... | conditional | flops 5000999936 | bytes 124396568 | solution.py:380
  7.1 5.2 %branch_0_fun.6 = (bf16[24,128,128]{2,1,0:T(8,128)(2,1)}, bf16[22,128,128]{2,1,0:T(8,128)(2,1)}, bf16[34,128,128]{2,1,0:T(8,128)(2,1)}, bf16[24,128,128]{2,1,0:T...) custom-call(s32[3,64]{1,0:T(4,128)S(1)} %get-tuple-element.94.refs_0_, ...), custom_call_target="tpu_custom_call" | custom-call | flops 1000000 | bytes 9830400 | tf_op jit(solution)/shard_map/cond/branch_0_fun/pallas_call | solution.py:94
  12.3 1.3 %collective-permute-start = (bf16[34,128,128]{2,1,0:T(8,128)(2,1)}, bf16[34,128,128]{2,1,0:T(8,128)(2,1)S(1)}, u32[]{:S(2)}, u32[]{:S(2)}) collective-permute-start(bf16[34,128,128]{2,1,0:T(8,128)(2,1)} %get-tuple-element.109), channel_id=1, source_target_pairs={{0,2},{1,3},{2,0},{3,1},{4,6},{5,7},{6,4},{7,5},{8,10},{9,11},{10,... | collective-permute-start | bytes 3342344 | tf_op jit(solution)/shard_map/cond/branch_0_fun/ppermute | solution.py:31
  13.6 1.5 %collective-permute-start.2 = (bf16[22,128,128]{2,1,0:T(8,128)(2,1)}, bf16[22,128,128]{2,1,0:T(8,128)(2,1)}, u32[]{:S(2)}, u32[]{:S(2)}) collective-permute-start(bf16[22,128,128]{2,1,0:T(8,128)(2,1)} %get-tuple-element.112), channel_id=1, source_target_pairs={{3,7},{7,11},{11,15},{19,23},{23,27},{27,31}} | collective-permute-start | bytes 2162696 | tf_op jit(solution)/shard_map/cond/branch_0_fun/ppermute | solution.py:31
  16.3 1.5 %collective-permute-start.4 = (bf16[20,128,128]{2,1,0:T(8,128)(2,1)}, bf16[20,128,128]{2,1,0:T(8,128)(2,1)}, u32[]{:S(2)}, u32[]{:S(2)}) collective-permute-start(bf16[20,128,128]{2,1,0:T(8,128)(2,1)} %get-tuple-element.114), channel_id=1, source_target_pairs={{3,7},{7,11},{11,15},{19,23},{23,27},{27,31}} | collective-permute-start | bytes 1966088 | tf_op jit(solution)/shard_map/cond/branch_0_fun/ppermute | solution.py:31
  17.8 1.3 %collective-permute-start.5 = (bf16[26,128,128]{2,1,0:T(8,128)(2,1)}, bf16[26,128,128]{2,1,0:T(8,128)(2,1)}, u32[]{:S(2)}, u32[]{:S(2)}) collective-permute-start(bf16[26,128,128]{2,1,0:T(8,128)(2,1)} %get-tuple-element.115), channel_id=1, source_target_pairs={{0,4},{1,5},{2,6},{4,8},{5,9},{6,10},{8,12},{9,13},{10,14},{16,20}... | collective-permute-start | bytes 2555912 | tf_op jit(solution)/shard_map/cond/branch_0_fun/ppermute | solution.py:31
  19.1 2.2 %collective-permute-start.3 = (bf16[24,128,128]{2,1,0:T(8,128)(2,1)}, bf16[24,128,128]{2,1,0:T(8,128)(2,1)}, u32[]{:S(2)}, u32[]{:S(2)}) collective-permute-start(bf16[24,128,128]{2,1,0:T(8,128)(2,1)} %get-tuple-element.113), channel_id=1, source_target_pairs={{0,1},{1,0},{2,3},{4,5},{5,4},{6,7},{8,9},{9,8},{10,11},{12,13},{1... | collective-permute-start | bytes 2359304 | tf_op jit(solution)/shard_map/cond/branch_0_fun/ppermute | solution.py:31
  21.3 12.8 %collective-permute-done.1.refs_5_ = bf16[24,128,128]{2,1,0:T(8,128)(2,1)} collective-permute-done((bf16[24,128,128]{2,1,0:T(8,128)(2,1)}, bf16[24,128,128]{2,1,0:T(8,128)(2,1)}, u32[]{:S(2)}, u32[]{:S(2)}) %collective-permute-start.1) | collective-permute-done | bytes 786464 | tf_op jit(solution)/shard_map/cond/branch_0_fun/ppermute | solution.py:31
  34.1 1.3 %collective-permute-start.8 = (bf16[22,128,128]{2,1,0:T(8,128)(2,1)}, bf16[22,128,128]{2,1,0:T(8,128)(2,1)}, u32[]{:S(2)}, u32[]{:S(2)}) collective-permute-start(bf16[22,128,128]{2,1,0:T(8,128)(2,1)} %collective-permute-done.2.refs_6_), channel_id=1, source_target_pairs={{3,0},{7,4},{11,8},{15,12},{19,16},{23,20},{27,24},{31,28}} | collective-permute-start | bytes 2162696 | tf_op jit(solution)/shard_map/cond/branch_0_fun/ppermute | solution.py:31
  35.4 3.2 %collective-permute-done.refs_7_ = bf16[34,128,128]{2,1,0:T(8,128)(2,1)S(1)} collective-permute-done((bf16[34,128,128]{2,1,0:T(8,128)(2,1)}, bf16[34,128,128]{2,1,0:T(8,128)(2,1)S(1)}, u32[]{:S(2)}, u32[]{:S(2)}) %collective-permute-start) | collective-permute-done | bytes 1114144 | tf_op jit(solution)/shard_map/cond/branch_0_fun/ppermute | solution.py:31
  38.6 4.1 %collective-permute-start.6 = (bf16[24,128,128]{2,1,0:T(8,128)(2,1)}, bf16[24,128,128]{2,1,0:T(8,128)(2,1)}, u32[]{:S(2)}, u32[]{:S(2)}) collective-permute-start(bf16[24,128,128]{2,1,0:T(8,128)(2,1)} %collective-permute-done.1.refs_5_), channel_id=1, source_target_pairs={{0,2},{1,3},{4,6},{5,7},{8,10},{9,11},{12,14},{13,15},{16,18},{17,... | collective-permute-start | bytes 2359304 | tf_op jit(solution)/shard_map/cond/branch_0_fun/ppermute | solution.py:31
  44.1 2.8 %branch_0_fun.7 = (s32[8,128]{1,0:T(8,128)}, s32[16,128]{1,0:T(8,128)}) custom-call(s32[16,128]{1,0:T(8,128)S(1)} %get-tuple-element.88.refs_0_, s32[16,128]{1,0:T(8,128)} %copy.122.refs_1_, s32[1,128]{1,0:T(1,128)S(1)} %get-tuple-element.92.refs_2_, s32[128,1]{1,0:T(8,128)} %copy.123.refs_3_, s32[1,128]{1,0:T(1,128)S(1)} %get-tuple-element.104.refs_4_, ...), custom_call_target="tpu_custom_call" | custom-call | flops 1000000000 | bytes 100000 | tf_op jit(solution)/shard_map/cond/branch_0_fun/pallas_call | solution.py:289
  47.5 6.0 %branch_0_fun.8.refs_2_ = f32[8,128]{1,0:T(8,128)} custom-call(s32[8,128]{1,0:T(8,128)} %get-tuple-element.107.refs_0_, s32[16,128]{1,0:T(8,128)} %get-tuple-element.108.refs_1_, f32[8,128]{1,0:T(8,128)} %broadcast_21_refs_2_.0.refs_2_, bf16[64,128,128]{2,1,0:T(8,128)(2,1)S(1)} %get-tuple-element.95.refs_1_.refs_3_, ...), custom_call_target="tpu_custom_call" | custom-call | flops 1000000000 | bytes 8000000 | tf_op jit(solution)/shard_map/cond/branch_0_fun/pallas_call | solution.py:161
  53.5 1.3 %collective-permute-start.10 = (bf16[34,128,128]{2,1,0:T(8,128)(2,1)S(1)}, bf16[34,128,128]{2,1,0:T(8,128)(2,1)}, u32[]{:S(2)}, u32[]{:S(2)}) collective-permute-start(bf16[34,128,128]{2,1,0:T(8,128)(2,1)S(1)} %collective-permute-done.refs_7_), channel_id=1, source_target_pairs={{0,4},{1,5},{4,8},{5,9},{8,12},{9,13},{16,20},{17,21},{20,24},{21,... | collective-permute-start | bytes 3342344 | tf_op jit(solution)/shard_map/cond/branch_0_fun/ppermute | solution.py:31
  54.8 1.3 %collective-permute-start.9 = (bf16[26,128,128]{2,1,0:T(8,128)(2,1)}, bf16[26,128,128]{2,1,0:T(8,128)(2,1)}, u32[]{:S(2)}, u32[]{:S(2)}) collective-permute-start(bf16[26,128,128]{2,1,0:T(8,128)(2,1)} %collective-permute-done.5.refs_10_), channel_id=1, source_target_pairs={{1,0},{2,1},{5,4},{6,5},{9,8},{10,9},{13,12},{14,13},{17,16},{18,1... | collective-permute-start | bytes 2555912 | tf_op jit(solution)/shard_map/cond/branch_0_fun/ppermute | solution.py:31
  56.2 1.6 %collective-permute-start.7 = (bf16[24,128,128]{2,1,0:T(8,128)(2,1)}, bf16[24,128,128]{2,1,0:T(8,128)(2,1)}, u32[]{:S(2)}, u32[]{:S(2)}) collective-permute-start(bf16[24,128,128]{2,1,0:T(8,128)(2,1)} %collective-permute-done.1.refs_5_), channel_id=1, source_target_pairs={{2,6},{6,10},{10,14},{18,22},{22,26},{26,30}} | collective-permute-start | bytes 2359304 | tf_op jit(solution)/shard_map/cond/branch_0_fun/ppermute | solution.py:31
  57.7 6.0 %collective-permute-start.12 = (bf16[24,128,128]{2,1,0:T(8,128)(2,1)}, bf16[24,128,128]{2,1,0:T(8,128)(2,1)}, u32[]{:S(2)}, u32[]{:S(2)}) collective-permute-start(bf16[24,128,128]{2,1,0:T(8,128)(2,1)} %collective-permute-done.3.refs_8_), channel_id=1, source_target_pairs={{0,2},{4,6},{8,10},{12,14},{16,18},{20,22},{24,26},{28,30}} | collective-permute-start | bytes 2359304 | tf_op jit(solution)/shard_map/cond/branch_0_fun/ppermute | solution.py:31
  63.7 1.3 %collective-permute-start.11 = (bf16[20,128,128]{2,1,0:T(8,128)(2,1)}, bf16[20,128,128]{2,1,0:T(8,128)(2,1)}, u32[]{:S(2)}, u32[]{:S(2)}) collective-permute-start(bf16[20,128,128]{2,1,0:T(8,128)(2,1)} %collective-permute-done.4.refs_9_), channel_id=1, source_target_pairs={{3,0},{7,4},{11,8},{15,12},{19,16},{23,20},{27,24},{31,28}} | collective-permute-start | bytes 1966088 | tf_op jit(solution)/shard_map/cond/branch_0_fun/ppermute | solution.py:31
  65.0 3.9 %branch_0_fun.9.refs_2_ = f32[8,128]{1,0:T(8,128)} custom-call(s32[8,128]{1,0:T(8,128)} %get-tuple-element.107.refs_0_, s32[16,128]{1,0:T(8,128)} %get-tuple-element.108.refs_1_, f32[8,128]{1,0:T(8,128)} %branch_0_fun.8.refs_2_, bf16[64,128,128]{2,1,0:T(8,128)(2,1)S(1)} %get-tuple-element.95.refs_1_.refs_3_, ...), custom_call_target="tpu_custom_call" | custom-call | flops 1000000000 | bytes 8000000 | tf_op jit(solution)/shard_map/cond/branch_0_fun/pallas_call | solution.py:161
  68.9 7.0 %collective-permute-done.9.refs_8_ = bf16[26,128,128]{2,1,0:T(8,128)(2,1)} collective-permute-done((bf16[26,128,128]{2,1,0:T(8,128)(2,1)}, bf16[26,128,128]{2,1,0:T(8,128)(2,1)}, u32[]{:S(2)}, u32[]{:S(2)}) %collective-permute-start.9) | collective-permute-done | bytes 852000 | tf_op jit(solution)/shard_map/cond/branch_0_fun/ppermute | solution.py:31
  75.9 4.1 %collective-permute-done.10.refs_9_ = bf16[34,128,128]{2,1,0:T(8,128)(2,1)} collective-permute-done((bf16[34,128,128]{2,1,0:T(8,128)(2,1)S(1)}, bf16[34,128,128]{2,1,0:T(8,128)(2,1)}, u32[]{:S(2)}, u32[]{:S(2)}) %collective-permute-start.10) | collective-permute-done | bytes 1114144 | tf_op jit(solution)/shard_map/cond/branch_0_fun/ppermute | solution.py:31
  80.0 7.6 %branch_0_fun.10.refs_2_ = f32[8,128]{1,0:T(8,128)} custom-call(s32[8,128]{1,0:T(8,128)} %get-tuple-element.107.refs_0_, s32[16,128]{1,0:T(8,128)} %get-tuple-element.108.refs_1_, f32[8,128]{1,0:T(8,128)} %branch_0_fun.9.refs_2_, bf16[64,128,128]{2,1,0:T(8,128)(2,1)S(1)} %get-tuple-element.95.refs_1_.refs_3_, ...), custom_call_target="tpu_custom_call" | custom-call | flops 1000000000 | bytes 8000000 | tf_op jit(solution)/shard_map/cond/branch_0_fun/pallas_call | solution.py:161
  87.6 3.7 %branch_0_fun.11 = f32[8,128]{1,0:T(8,128)S(1)} custom-call(s32[8,128]{1,0:T(8,128)} %get-tuple-element.107.refs_0_, s32[16,128]{1,0:T(8,128)} %get-tuple-element.108.refs_1_, f32[8,128]{1,0:T(8,128)} %branch_0_fun.10.refs_2_, bf16[64,128,128]{2,1,0:T(8,128)(2,1)S(1)} %get-tuple-element.95.refs_1_.refs_3_, ...), custom_call_target="tpu_custom_call" | custom-call | flops 1000000000 | bytes 8000000 | tf_op jit(solution)/shard_map/cond/branch_0_fun/pallas_call | solution.py:161
  91.6 2.5 %collective-permute-start.49 = (f32[8,64]{1,0:T(8,128)S(1)}, f32[8,64]{1,0:T(8,128)S(1)}, u32[]{:S(2)}, u32[]{:S(2)}) collective-permute-start(f32[8,64]{1,0:T(8,128)S(1)} %constant_dynamic-slice_fusion), channel_id=1, source_target_pairs={{0,16},{16,0},{1,17},{17,1},{2,18},{18,2},{3,19},{19,3},{4,20},{20... | collective-permute-start | bytes 6152 | tf_op jit(solution)/shard_map/ppermute | solution.py:25
  (81 shorter events, 11.0 us)
Async XLA Ops:
  0.0 5.3 %copy-start.5 = (s32[3,16,4]{1,2,0:T(4,128)S(1)}, s32[3,16,4]{1,2,0:T(4,128)}, u32[]{:S(2)}) copy-start(s32[3,16,4]{1,2,0:T(4,128)} %constant.221.clone) | copy-start | bytes 2308
  0.0 7.1 %copy-start = (bf16[8,8,128,128]{3,2,1,0:T(8,128)(2,1)S(1)}, bf16[8,8,128,128]{3,2,1,0:T(8,128)(2,1)}, u32[]{:S(2)}) copy-start(bf16[8,8,128,128]{3,2,1,0:T(8,128)(2,1)} %param.7) | copy-start | bytes 6291460
  0.0 4.0 %copy-start.4 = (s32[128,16]{0,1:T(8,128)S(1)}, s32[128,16]{0,1:T(8,128)}, u32[]{:S(2)}) copy-start(s32[128,16]{0,1:T(8,128)} %param.8) | copy-start | bytes 24580
  0.0 7.1 %collective-permute-start.48 = (bf16[64,128,128]{2,1,0:T(8,128)(2,1)}, bf16[64,128,128]{2,1,0:T(8,128)(2,1)}, u32[]{:S(2)}, u32[]{:S(2)}) collective-permute-start(bf16[64,128,128]{2,1,0:T(8,128)(2,1)} %bitcast.40), channel_id=1, source_target_pairs={{0,16},{16,0},{1,17},{17,1},{2,18},{18,2},{3,19},{19,3},{4,20},{20... | collective-permute-start | bytes 6291464 | tf_op jit(solution)/shard_map/ppermute | solution.py:25
  12.3 26.4 %collective-permute-start = (bf16[34,128,128]{2,1,0:T(8,128)(2,1)}, bf16[34,128,128]{2,1,0:T(8,128)(2,1)S(1)}, u32[]{:S(2)}, u32[]{:S(2)}) collective-permute-start(bf16[34,128,128]{2,1,0:T(8,128)(2,1)} %get-tuple-element.109), channel_id=1, source_target_pairs={{0,2},{1,3},{2,0},{3,1},{4,6},{5,7},{6,4},{7,5},{8,10},{9,11},{10,... | collective-permute-start | bytes 3342344 | tf_op jit(solution)/shard_map/cond/branch_0_fun/ppermute | solution.py:31
  13.6 5.5 %collective-permute-start.2 = (bf16[22,128,128]{2,1,0:T(8,128)(2,1)}, bf16[22,128,128]{2,1,0:T(8,128)(2,1)}, u32[]{:S(2)}, u32[]{:S(2)}) collective-permute-start(bf16[22,128,128]{2,1,0:T(8,128)(2,1)} %get-tuple-element.112), channel_id=1, source_target_pairs={{3,7},{7,11},{11,15},{19,23},{23,27},{27,31}} | collective-permute-start | bytes 2162696 | tf_op jit(solution)/shard_map/cond/branch_0_fun/ppermute | solution.py:31
  15.1 19.0 %collective-permute-start.1 = (bf16[24,128,128]{2,1,0:T(8,128)(2,1)}, bf16[24,128,128]{2,1,0:T(8,128)(2,1)}, u32[]{:S(2)}, u32[]{:S(2)}) collective-permute-start(bf16[24,128,128]{2,1,0:T(8,128)(2,1)} %get-tuple-element.111), channel_id=1, source_target_pairs={{0,1},{1,0},{2,3},{3,2},{4,5},{5,4},{6,7},{7,6},{8,9},{9,8},{10,11... | collective-permute-start | bytes 2359304 | tf_op jit(solution)/shard_map/cond/branch_0_fun/ppermute | solution.py:31
  16.3 37.2 %collective-permute-start.4 = (bf16[20,128,128]{2,1,0:T(8,128)(2,1)}, bf16[20,128,128]{2,1,0:T(8,128)(2,1)}, u32[]{:S(2)}, u32[]{:S(2)}) collective-permute-start(bf16[20,128,128]{2,1,0:T(8,128)(2,1)} %get-tuple-element.114), channel_id=1, source_target_pairs={{3,7},{7,11},{11,15},{19,23},{23,27},{27,31}} | collective-permute-start | bytes 1966088 | tf_op jit(solution)/shard_map/cond/branch_0_fun/ppermute | solution.py:31
  17.8 37.0 %collective-permute-start.5 = (bf16[26,128,128]{2,1,0:T(8,128)(2,1)}, bf16[26,128,128]{2,1,0:T(8,128)(2,1)}, u32[]{:S(2)}, u32[]{:S(2)}) collective-permute-start(bf16[26,128,128]{2,1,0:T(8,128)(2,1)} %get-tuple-element.115), channel_id=1, source_target_pairs={{0,4},{1,5},{2,6},{4,8},{5,9},{6,10},{8,12},{9,13},{10,14},{16,20}... | collective-permute-start | bytes 2555912 | tf_op jit(solution)/shard_map/cond/branch_0_fun/ppermute | solution.py:31
  19.1 37.0 %collective-permute-start.3 = (bf16[24,128,128]{2,1,0:T(8,128)(2,1)}, bf16[24,128,128]{2,1,0:T(8,128)(2,1)}, u32[]{:S(2)}, u32[]{:S(2)}) collective-permute-start(bf16[24,128,128]{2,1,0:T(8,128)(2,1)} %get-tuple-element.113), channel_id=1, source_target_pairs={{0,1},{1,0},{2,3},{4,5},{5,4},{6,7},{8,9},{9,8},{10,11},{12,13},{1... | collective-permute-start | bytes 2359304 | tf_op jit(solution)/shard_map/cond/branch_0_fun/ppermute | solution.py:31
  34.1 23.6 %collective-permute-start.8 = (bf16[22,128,128]{2,1,0:T(8,128)(2,1)}, bf16[22,128,128]{2,1,0:T(8,128)(2,1)}, u32[]{:S(2)}, u32[]{:S(2)}) collective-permute-start(bf16[22,128,128]{2,1,0:T(8,128)(2,1)} %collective-permute-done.2.refs_6_), channel_id=1, source_target_pairs={{3,0},{7,4},{11,8},{15,12},{19,16},{23,20},{27,24},{31,28}} | collective-permute-start | bytes 2162696 | tf_op jit(solution)/shard_map/cond/branch_0_fun/ppermute | solution.py:31
  38.6 14.9 %copy-start.3 = (bf16[34,128,128]{2,1,0:T(8,128)(2,1)}, bf16[34,128,128]{2,1,0:T(8,128)(2,1)S(1)}, u32[]{:S(2)}) copy-start(bf16[34,128,128]{2,1,0:T(8,128)(2,1)S(1)} %collective-permute-done.refs_7_) | copy-start | bytes 3342340 | tf_op jit(solution)/shard_map/cond
  38.6 25.1 %collective-permute-start.6 = (bf16[24,128,128]{2,1,0:T(8,128)(2,1)}, bf16[24,128,128]{2,1,0:T(8,128)(2,1)}, u32[]{:S(2)}, u32[]{:S(2)}) collective-permute-start(bf16[24,128,128]{2,1,0:T(8,128)(2,1)} %collective-permute-done.1.refs_5_), channel_id=1, source_target_pairs={{0,2},{1,3},{4,6},{5,7},{8,10},{9,11},{12,14},{13,15},{16,18},{17,... | collective-permute-start | bytes 2359304 | tf_op jit(solution)/shard_map/cond/branch_0_fun/ppermute | solution.py:31
  53.5 26.5 %collective-permute-start.10 = (bf16[34,128,128]{2,1,0:T(8,128)(2,1)S(1)}, bf16[34,128,128]{2,1,0:T(8,128)(2,1)}, u32[]{:S(2)}, u32[]{:S(2)}) collective-permute-start(bf16[34,128,128]{2,1,0:T(8,128)(2,1)S(1)} %collective-permute-done.refs_7_), channel_id=1, source_target_pairs={{0,4},{1,5},{4,8},{5,9},{8,12},{9,13},{16,20},{17,21},{20,24},{21,... | collective-permute-start | bytes 3342344 | tf_op jit(solution)/shard_map/cond/branch_0_fun/ppermute | solution.py:31
  54.8 21.1 %collective-permute-start.9 = (bf16[26,128,128]{2,1,0:T(8,128)(2,1)}, bf16[26,128,128]{2,1,0:T(8,128)(2,1)}, u32[]{:S(2)}, u32[]{:S(2)}) collective-permute-start(bf16[26,128,128]{2,1,0:T(8,128)(2,1)} %collective-permute-done.5.refs_10_), channel_id=1, source_target_pairs={{1,0},{2,1},{5,4},{6,5},{9,8},{10,9},{13,12},{14,13},{17,16},{18,1... | collective-permute-start | bytes 2555912 | tf_op jit(solution)/shard_map/cond/branch_0_fun/ppermute | solution.py:31
  56.2 12.8 %collective-permute-start.7 = (bf16[24,128,128]{2,1,0:T(8,128)(2,1)}, bf16[24,128,128]{2,1,0:T(8,128)(2,1)}, u32[]{:S(2)}, u32[]{:S(2)}) collective-permute-start(bf16[24,128,128]{2,1,0:T(8,128)(2,1)} %collective-permute-done.1.refs_5_), channel_id=1, source_target_pairs={{2,6},{6,10},{10,14},{18,22},{22,26},{26,30}} | collective-permute-start | bytes 2359304 | tf_op jit(solution)/shard_map/cond/branch_0_fun/ppermute | solution.py:31
  57.7 29.9 %collective-permute-start.12 = (bf16[24,128,128]{2,1,0:T(8,128)(2,1)}, bf16[24,128,128]{2,1,0:T(8,128)(2,1)}, u32[]{:S(2)}, u32[]{:S(2)}) collective-permute-start(bf16[24,128,128]{2,1,0:T(8,128)(2,1)} %collective-permute-done.3.refs_8_), channel_id=1, source_target_pairs={{0,2},{4,6},{8,10},{12,14},{16,18},{20,22},{24,26},{28,30}} | collective-permute-start | bytes 2359304 | tf_op jit(solution)/shard_map/cond/branch_0_fun/ppermute | solution.py:31
  63.7 23.9 %collective-permute-start.11 = (bf16[20,128,128]{2,1,0:T(8,128)(2,1)}, bf16[20,128,128]{2,1,0:T(8,128)(2,1)}, u32[]{:S(2)}, u32[]{:S(2)}) collective-permute-start(bf16[20,128,128]{2,1,0:T(8,128)(2,1)} %collective-permute-done.4.refs_9_), channel_id=1, source_target_pairs={{3,0},{7,4},{11,8},{15,12},{19,16},{23,20},{27,24},{31,28}} | collective-permute-start | bytes 1966088 | tf_op jit(solution)/shard_map/cond/branch_0_fun/ppermute | solution.py:31
  91.6 3.4 %collective-permute-start.49 = (f32[8,64]{1,0:T(8,128)S(1)}, f32[8,64]{1,0:T(8,128)S(1)}, u32[]{:S(2)}, u32[]{:S(2)}) collective-permute-start(f32[8,64]{1,0:T(8,128)S(1)} %constant_dynamic-slice_fusion), channel_id=1, source_target_pairs={{0,16},{16,0},{1,17},{17,1},{2,18},{18,2},{3,19},{19,3},{4,20},{20... | collective-permute-start | bytes 6152 | tf_op jit(solution)/shard_map/ppermute | solution.py:25
